TPU v7x, 32 devices: a whole 2x2x4 slice. The times are simulated.
32 devices in a mesh: rep: 2 (over x), mp: 4 (over z), tok: 4 (over y, core).
Axes of the slice: x: 2, y: 2, z: 4, core: 2. Of those that a mesh axis runs over, the one named last changes fastest.
Arguments:
- hidden_in: bfloat16 [8192, 1536], P(('rep', 'tok', 'mp')), parts along dimension 0
- seg_ids: int32 [8192], P(('rep', 'tok', 'mp')), parts along dimension 0
- expert_ids: int32 [8192, 2], P(('rep', 'tok', 'mp')), parts along dimension 0
- expert_gates: float32 [8192, 2], P(('rep', 'tok', 'mp')), parts along dimension 0
- w_query: bfloat16 [2, 1536, 24, 64], P(None, 'tok', 'mp')
- w_key: bfloat16 [2, 1536, 8, 64], P(None, 'tok', 'mp')
- w_value: bfloat16 [2, 1536, 8, 64], P(None, 'tok', 'mp')
- w_out: bfloat16 [2, 24, 64, 1536], P(None, 'mp', None, 'tok')
- w_gate: bfloat16 [2, 40, 1536, 512], P(None, None, 'tok', 'mp')
- w_up: bfloat16 [2, 40, 1536, 512], P(None, None, 'tok', 'mp')
- w_down: bfloat16 [2, 40, 512, 1536], P(None, None, 'mp', 'tok')
- gain_attn: bfloat16 [2, 1536], replicated
- gain_mlp: bfloat16 [2, 1536], replicated
Outputs:
- output: float32 [8192, 1536], P(('rep', 'tok', 'mp')), parts along dimension 0
There are 2 independent parts. A program takes and returns all parts, laid end to end along the dimension named above; an argument that names none is the same for every part.
All inputs are finite; a program needn't handle non-finite values.
Results may differ from a plain program's by a relative error of at most 0.0149105.
Values are sent between devices in bfloat16 or wider.
A program may use at most 1 GiB of HBM per device.

v0:
```python
import jax
import jax.numpy as jnp
from jax import lax
from jax.sharding import PartitionSpec as P

EPS = 1e-5
ROPE_BASE = 10000.0


def rms_norm(residual, gain):
    inv_rms = lax.rsqrt(jnp.mean(residual * residual, axis=-1, keepdims=True) + EPS)
    return (residual * inv_rms * gain.astype(jnp.float32)).astype(jnp.bfloat16)


def request_positions(seg_rows):
    token_index = jnp.arange(seg_rows.shape[-1], dtype=jnp.int32)
    is_start = jnp.concatenate([jnp.ones(seg_rows.shape[:-1] + (1,), dtype=jnp.bool_), seg_rows[..., 1:] != seg_rows[..., :-1]], axis=-1)
    start_index = lax.cummax(jnp.where(is_start, token_index, 0), axis=seg_rows.ndim - 1)
    return token_index - start_index


def rope_tables(positions, head_dim):
    inv_freq = jnp.power(ROPE_BASE, -jnp.arange(head_dim // 2, dtype=jnp.float32) * 2.0 / head_dim)
    angles = positions.astype(jnp.float32)[..., None] * inv_freq
    return jnp.cos(angles)[..., None, :], jnp.sin(angles)[..., None, :]


def apply_rope(vectors, cosines, sines):
    half_dim = vectors.shape[-1] // 2
    first_half = vectors[..., :half_dim]
    second_half = vectors[..., half_dim:]
    return jnp.concatenate([first_half * cosines - second_half * sines, second_half * cosines + first_half * sines], axis=-1)


def block_attention(q_rot, k_rot, v_all, seg_query, query_index, seg_keys, key_index):
    n_query, kv_heads, groups, head_dim = q_rot.shape
    block = min(n_query, 512)
    num_blocks = n_query // block
    scale = head_dim ** -0.5

    def one_block(block_in):
        q_block, seg_block, index_block = block_in
        scores = jnp.einsum('bhgd,shd->hgbs', q_block, k_rot, preferred_element_type=jnp.float32) * scale
        allowed = (seg_block[:, None] == seg_keys[None, :]) & (key_index[None, :] <= index_block[:, None])
        attn_prob = jax.nn.softmax(jnp.where(allowed, scores, -1e30), axis=-1).astype(jnp.bfloat16)
        return jnp.einsum('hgbs,shd->bhgd', attn_prob, v_all, preferred_element_type=jnp.float32).astype(jnp.bfloat16)

    block_outs = lax.map(one_block, (q_rot.reshape(num_blocks, block, kv_heads, groups, head_dim), seg_query.reshape(num_blocks, block), query_index.reshape(num_blocks, block)))
    return block_outs.reshape(n_query, kv_heads * groups, head_dim)


def expert_mix(normed, pair_token, pair_gate, group_sizes, gate_weight, up_weight, down_weight):
    pair_rows = normed[pair_token]
    gate_pre = lax.ragged_dot(pair_rows, gate_weight, group_sizes, preferred_element_type=jnp.float32)
    up_pre = lax.ragged_dot(pair_rows, up_weight, group_sizes, preferred_element_type=jnp.float32)
    hidden_act = (jax.nn.silu(gate_pre) * up_pre).astype(jnp.bfloat16)
    down_out = lax.ragged_dot(hidden_act, down_weight, group_sizes, preferred_element_type=jnp.float32)
    return jax.ops.segment_sum(down_out * pair_gate[:, None], pair_token, num_segments=normed.shape[0])


def solution(mesh):
    token_spec = P(('rep', 'tok', 'mp'))
    row_spec = P(('rep', 'tok', 'mp'), None)
    head_weight = P(None, 'tok', 'mp', None)
    in_specs = (row_spec, token_spec, row_spec, row_spec, head_weight, head_weight, head_weight, P(None, 'mp', None, 'tok'), P(None, None, 'tok', 'mp'), P(None, None, 'tok', 'mp'), P(None, None, 'mp', 'tok'), P(None, None), P(None, None))

    def device_step(hidden_in, seg_ids, expert_ids, expert_gates, w_query, w_key, w_value, w_out, w_gate, w_up, w_down, gain_attn, gain_mlp):
        num_layers, _, q_local, head_dim = w_query.shape
        kv_local = w_key.shape[2]
        groups = q_local // kv_local
        num_experts = w_gate.shape[1]
        seg_full = lax.all_gather(seg_ids, 'mp', axis=0, tiled=True)
        ids_full = lax.all_gather(expert_ids, 'mp', axis=0, tiled=True)
        gates_full = lax.all_gather(expert_gates, 'mp', axis=0, tiled=True)
        seq_len = seg_full.shape[0]
        token_index = jnp.arange(seq_len, dtype=jnp.int32)
        cosines, sines = rope_tables(request_positions(seg_full), head_dim)
        flat_ids = ids_full.reshape(2 * seq_len)
        pair_order = jnp.argsort(flat_ids, stable=True)
        group_sizes = jnp.bincount(flat_ids, length=num_experts).astype(jnp.int32)
        pair_token = pair_order // 2
        pair_gate = gates_full.reshape(2 * seq_len)[pair_order]
        residual = hidden_in.astype(jnp.float32)
        for layer in range(num_layers):
            q_weight = lax.all_gather(w_query[layer], 'tok', axis=0, tiled=True)
            k_weight = lax.all_gather(w_key[layer], 'tok', axis=0, tiled=True)
            v_weight = lax.all_gather(w_value[layer], 'tok', axis=0, tiled=True)
            o_weight = lax.all_gather(w_out[layer], 'tok', axis=2, tiled=True)
            gate_weight = lax.all_gather(w_gate[layer], 'tok', axis=1, tiled=True)
            up_weight = lax.all_gather(w_up[layer], 'tok', axis=1, tiled=True)
            down_weight = lax.all_gather(w_down[layer], 'tok', axis=2, tiled=True)
            normed = lax.all_gather(rms_norm(residual, gain_attn[layer]), 'mp', axis=0, tiled=True)
            q_proj = jnp.einsum('se,ehd->shd', normed, q_weight, preferred_element_type=jnp.float32)
            k_proj = jnp.einsum('se,ehd->shd', normed, k_weight, preferred_element_type=jnp.float32)
            v_proj = jnp.einsum('se,ehd->shd', normed, v_weight, preferred_element_type=jnp.float32)
            q_rot = apply_rope(q_proj, cosines, sines).astype(jnp.bfloat16).reshape(seq_len, kv_local, groups, head_dim)
            k_rot = apply_rope(k_proj, cosines, sines).astype(jnp.bfloat16)
            attn_out = block_attention(q_rot, k_rot, v_proj.astype(jnp.bfloat16), seg_full, token_index, seg_full, token_index)
            attn_part = jnp.einsum('shd,hde->se', attn_out, o_weight, preferred_element_type=jnp.float32)
            residual = residual + lax.psum_scatter(attn_part, 'mp', scatter_dimension=0, tiled=True)
            normed = lax.all_gather(rms_norm(residual, gain_mlp[layer]), 'mp', axis=0, tiled=True)
            mix_part = expert_mix(normed, pair_token, pair_gate, group_sizes, gate_weight, up_weight, down_weight)
            residual = residual + lax.psum_scatter(mix_part, 'mp', scatter_dimension=0, tiled=True)
        return residual

    return jax.shard_map(device_step, mesh=mesh, in_specs=in_specs, out_specs=row_spec, check_vma=False)
```

profile of v0, /device:TPU:0, one launch (start us, length us, event | category | flops | bytes accessed | tf_op | source)
XLA Modules:
  0.0 1606.1 jit_solution(702387391607951561)
XLA Ops:
  14.8 12.7 all-gather.14
  28.9 6.5 all-gather.1
  36.0 6.5 all-gather.2
  43.1 50.2 %all-gather.30.cloned.1.call-done = bf16[1024,1536]{1,0:T(8,128)(2,1)} async-done(((bf16[256,1536]{1,0:T(8,128)(2,1)}), bf16[1024,1536]{1,0:T(8,128)(2,1)}) %all-gather.30.cloned.1.call-update) | async-done | bytes 3145744 | tf_op jit(solution)/shard_map/all_gather | solution.py:92
  108.7 29.4 %while.22 = (s32[]{:T(128)}, bf16[2,512,2,3,64]{1,4,3,2,0:T(8,128)(2,1)S(1)}, s32[2,512]{1,0:T(2,128)S(1)}, s32[1024]{0:T(1024)S(1)}, s32[2,512]{1,0:T(2,128)S(1...) while((s32[]{:T(128)}, ...), condition=%wide.region_6.7_spmd.clone, body=%wide.region_3.6_spmd.clone.sunk | while | flops 825951232 | bytes 27570280 | solution.py:48
  109.3 7.4 fusion.161
  116.8 6.7 fusion.162
  124.1 7.4 fusion.161
  131.5 6.7 fusion.162
  139.6 5.7 convolution_bitcast_fusion.1
  146.6 108.3 %reduce-scatter.5.cloned.1.call-done = f32[256,1536]{1,0:T(8,128)} async-done(((f32[1024,1536]{1,0:T(8,128)}), f32[256,1536]{1,0:T(8,128)}) %reduce-scatter.5.cloned.1.call-update) | async-done | bytes 1572880 | tf_op jit(solution)/shard_map/reduce_scatter | solution.py:100
  258.0 5.8 fusion.119
  263.9 5.7 fusion.120
  269.7 5.9 fusion.118
  276.3 13.7 all_gather.69
  291.0 15.3 scatter_custom_fusion
  308.9 13.3 all_gather.74
  327.8 11.8 gather_fusion.1
  339.7 15.7 gather_fusion
  355.3 70.2 %all-gather.42.cloned.1.call-done = bf16[1,40,1536,128]{3,2,1,0:T(8,128)(2,1)} async-done(((bf16[1,40,384,128]{3,2,1,0:T(8,128)(2,1)}), bf16[1,40,1536,128]{3,2,1,0:T(8,128)(2,1)}) %all-gather.42.cloned.1.call-update) | async-done | bytes 15728656 | tf_op jit(solution)/shard_map/all_gather | solution.py:89
  425.5 36.3 %ragged-dot-none.5 = f32[2048,128]{1,0:T(8,128)} custom-call(s32[1]{0:T(128)} %get-tuple-element.115, s32[41]{0:T(128)} %get-tuple-element.116, s32[47]{0:T(128)} %get-tuple-element.117, s32[47]{0:T(128)} %get-tuple-element.118, s32[1]{0:T(128)} %get-tuple-element.115, bf16[2048,1536]{1,0:T(8,128)(2,1)} %gather_fusion, bf16[40,1536,128]{2,1,0:T(8,128)(2,1)} %bitcast.204), custom_call_target="tpu_custom_call" | custom-call | flops 805306368 | bytes 23068832 | tf_op jit(solution)/shard_map/ragged_dot_general/ragged-dot-none
  461.8 66.2 %all-gather.44.cloned.1.call-done = bf16[1,40,1536,128]{3,2,1,0:T(8,128)(2,1)} async-done(((bf16[1,40,384,128]{3,2,1,0:T(8,128)(2,1)}), bf16[1,40,1536,128]{3,2,1,0:T(8,128)(2,1)}) %all-gather.44.cloned.1.call-update) | async-done | bytes 15728656 | tf_op jit(solution)/shard_map/all_gather | solution.py:90
  528.0 36.4 %ragged-dot-none.4 = f32[2048,128]{1,0:T(8,128)} custom-call(s32[1]{0:T(128)} %get-tuple-element.115, s32[41]{0:T(128)} %get-tuple-element.116, s32[47]{0:T(128)} %get-tuple-element.117, s32[47]{0:T(128)} %get-tuple-element.118, s32[1]{0:T(128)} %get-tuple-element.115, bf16[2048,1536]{1,0:T(8,128)(2,1)} %gather_fusion, bf16[40,1536,128]{2,1,0:T(8,128)(2,1)} %bitcast.205), custom_call_target="tpu_custom_call" | custom-call | flops 805306368 | bytes 23068832 | tf_op jit(solution)/shard_map/ragged_dot_general/ragged-dot-none
  566.7 63.6 %all-gather.46.cloned.1.call-done = bf16[1,40,128,1536]{3,2,1,0:T(8,128)(2,1)} async-done(((bf16[1,40,128,384]{3,2,1,0:T(8,128)(2,1)}), bf16[1,40,128,1536]{3,2,1,0:T(8,128)(2,1)}) %all-gather.46.cloned.1.call-update) | async-done | bytes 15728656 | tf_op jit(solution)/shard_map/all_gather | solution.py:91
  630.3 37.9 %ragged-dot-none.3 = f32[2048,1536]{1,0:T(8,128)} custom-call(s32[1]{0:T(128)} %get-tuple-element.115, s32[41]{0:T(128)} %get-tuple-element.116, s32[47]{0:T(128)} %get-tuple-element.117, s32[47]{0:T(128)} %get-tuple-element.118, s32[1]{0:T(128)} %get-tuple-element.115, bf16[2048,128]{1,0:T(8,128)(2,1)} %multiply_convert_fusion.4, ...), custom_call_target="tpu_custom_call" | custom-call | flops 805306368 | bytes 28836000 | tf_op jit(solution)/shard_map/ragged_dot_general/ragged-dot-none
  668.2 25.7 %scatter_custom_fusion.1 = f32[1024,1536]{1,0:T(8,128)} fusion(s32[2048]{0:T(1024)S(1)} %get-tuple-element.235, f32[2048,1536]{1,0:T(8,128)} %ragged-dot-none.3, f32[2048]{0:T(1024)S(1)} %gather_fusion.1, f32[]{:T(128)} %constant.82.clone.1), kind=kCustom, calls=%fused_computation.72 | custom fusion | flops 6291456 | bytes 18882564 | tf_op jit(solution)/shard_map/scatter-add | solution.py:58
  694.0 111.9 %reduce-scatter.7.cloned.1.call-done = f32[256,1536]{1,0:T(8,128)} async-done(((f32[1024,1536]{1,0:T(8,128)}), f32[256,1536]{1,0:T(8,128)}) %reduce-scatter.7.cloned.1.call-update) | async-done | bytes 1572880 | tf_op jit(solution)/shard_map/reduce_scatter | solution.py:103
  811.4 6.4 all-gather.8
  817.8 6.9 all-gather.9
  824.7 49.0 %all-gather.34.cloned.1.call-done = bf16[1024,1536]{1,0:T(8,128)(2,1)} async-done(((bf16[256,1536]{1,0:T(8,128)(2,1)}), bf16[1024,1536]{1,0:T(8,128)(2,1)}) %all-gather.34.cloned.1.call-update) | async-done | bytes 3145744 | tf_op jit(solution)/shard_map/all_gather | solution.py:92
  877.7 13.6 all-gather.48.cloned.1.call-done
  901.0 29.4 %while.23 = (s32[]{:T(128)}, bf16[2,512,2,3,64]{1,4,3,2,0:T(8,128)(2,1)S(1)}, s32[2,512]{1,0:T(2,128)S(1)}, s32[1024]{0:T(1024)S(1)}, s32[2,512]{1,0:T(2,128)S(1...) while((s32[]{:T(128)}, ...), condition=%wide.region_17.18_spmd.clone, body=%wide.region_14.17_spmd.clone.sunk | while | flops 825951232 | bytes 27570280 | solution.py:48
  901.6 7.4 fusion.167
  909.1 6.7 fusion.168
  916.3 7.4 fusion.167
  923.8 6.7 fusion.168
  931.9 5.7 convolution_bitcast_fusion
  937.7 110.6 %reduce-scatter.9.cloned.1.call-done = f32[256,1536]{1,0:T(8,128)} async-done(((f32[1024,1536]{1,0:T(8,128)}), f32[256,1536]{1,0:T(8,128)}) %reduce-scatter.9.cloned.1.call-update) | async-done | bytes 1572880 | tf_op jit(solution)/shard_map/reduce_scatter | solution.py:100
  1053.2 61.6 %all-gather.36.cloned.1.call-done = bf16[1024,1536]{1,0:T(8,128)(2,1)} async-done(((bf16[256,1536]{1,0:T(8,128)(2,1)}), bf16[1024,1536]{1,0:T(8,128)(2,1)}) %all-gather.36.cloned.1.call-update) | async-done | bytes 3145744 | tf_op jit(solution)/shard_map/all_gather | solution.py:101
  1114.7 15.7 gather_fusion.2
  1130.4 85.5 %all-gather.52.cloned.1.call-done = bf16[1,40,1536,128]{3,2,1,0:T(8,128)(2,1)} async-done(((bf16[1,40,384,128]{3,2,1,0:T(8,128)(2,1)}), bf16[1,40,1536,128]{3,2,1,0:T(8,128)(2,1)}) %all-gather.52.cloned.1.call-update) | async-done | bytes 15728656 | tf_op jit(solution)/shard_map/all_gather | solution.py:89
  1215.9 36.3 %ragged-dot-none.2 = f32[2048,128]{1,0:T(8,128)} custom-call(s32[1]{0:T(128)} %get-tuple-element.115, s32[41]{0:T(128)} %get-tuple-element.116, s32[47]{0:T(128)} %get-tuple-element.117, s32[47]{0:T(128)} %get-tuple-element.118, s32[1]{0:T(128)} %get-tuple-element.115, bf16[2048,1536]{1,0:T(8,128)(2,1)} %gather_fusion.2, bf16[40,1536,128]{2,1,0:T(8,128)(2,1)} %bitcast.207), custom_call_target="tpu_custom_call" | custom-call | flops 805306368 | bytes 23068832 | tf_op jit(solution)/shard_map/ragged_dot_general/ragged-dot-none
  1252.2 66.1 %all-gather.54.cloned.1.call-done = bf16[1,40,1536,128]{3,2,1,0:T(8,128)(2,1)} async-done(((bf16[1,40,384,128]{3,2,1,0:T(8,128)(2,1)}), bf16[1,40,1536,128]{3,2,1,0:T(8,128)(2,1)}) %all-gather.54.cloned.1.call-update) | async-done | bytes 15728656 | tf_op jit(solution)/shard_map/all_gather | solution.py:90
  1318.3 36.4 %ragged-dot-none.1 = f32[2048,128]{1,0:T(8,128)} custom-call(s32[1]{0:T(128)} %get-tuple-element.115, s32[41]{0:T(128)} %get-tuple-element.116, s32[47]{0:T(128)} %get-tuple-element.117, s32[47]{0:T(128)} %get-tuple-element.118, s32[1]{0:T(128)} %get-tuple-element.115, bf16[2048,1536]{1,0:T(8,128)(2,1)} %gather_fusion.2, bf16[40,1536,128]{2,1,0:T(8,128)(2,1)} %bitcast.209), custom_call_target="tpu_custom_call" | custom-call | flops 805306368 | bytes 23068832 | tf_op jit(solution)/shard_map/ragged_dot_general/ragged-dot-none
  1357.0 63.5 %all-gather.56.cloned.1.call-done = bf16[1,40,128,1536]{3,2,1,0:T(8,128)(2,1)} async-done(((bf16[1,40,128,384]{3,2,1,0:T(8,128)(2,1)}), bf16[1,40,128,1536]{3,2,1,0:T(8,128)(2,1)}) %all-gather.56.cloned.1.call-update) | async-done | bytes 15728656 | tf_op jit(solution)/shard_map/all_gather | solution.py:91
  1420.4 37.9 %ragged-dot-none = f32[2048,1536]{1,0:T(8,128)} custom-call(s32[1]{0:T(128)} %get-tuple-element.115, s32[41]{0:T(128)} %get-tuple-element.116, s32[47]{0:T(128)} %get-tuple-element.117, s32[47]{0:T(128)} %get-tuple-element.118, s32[1]{0:T(128)} %get-tuple-element.115, bf16[2048,128]{1,0:T(8,128)(2,1)} %multiply_convert_fusion.3, bf16[40,128,1536]{2,1,0:T(8,128)(2,1)} %bitcast.208), custom_call_target="tpu_custom_call" | custom-call | flops 805306368 | bytes 28836000 | tf_op jit(solution)/shard_map/ragged_dot_general/ragged-dot-none
  1458.4 25.7 %scatter_custom_fusion.2 = f32[1024,1536]{1,0:T(8,128)} fusion(s32[2048]{0:T(1024)} %copy-done.29, f32[2048,1536]{1,0:T(8,128)} %ragged-dot-none, f32[2048]{0:T(1024)S(1)} %copy-done.23, f32[]{:T(128)} %constant.82.clone.1), kind=kCustom, calls=%fused_computation.70 | custom fusion | flops 6291456 | bytes 18883072 | tf_op jit(solution)/shard_map/scatter-add | solution.py:58
  1484.1 111.9 %reduce-scatter.11.cloned.1.call-done = f32[256,1536]{1,0:T(8,128)} async-done(((f32[1024,1536]{1,0:T(8,128)}), f32[256,1536]{1,0:T(8,128)}) %reduce-scatter.11.cloned.1.call-update) | async-done | bytes 1572880 | tf_op jit(solution)/shard_map/reduce_scatter | solution.py:103
  (189 shorter events, 76.9 us)
Async XLA Ops:
  6.5 7.2 copy-start.15
  6.5 8.2 copy-start.32
  6.5 21.7 %copy-start.20 = (bf16[2,384,2,64]{1,3,2,0:T(8,128)(2,1)S(1)}, bf16[2,384,2,64]{1,3,2,0:T(8,128)(2,1)}, u32[]{:S(2)}) copy-start(bf16[2,384,2,64]{1,3,2,0:T(8,128)(2,1)} %param.22) | copy-start | bytes 589828
  6.5 36.6 %all-gather.38.cloned.1.call-start = ((), (), s32[]{:S(2)}) async-start(), calls=%async_computation.12 | async-start | bytes 1474560 | tf_op jit(solution)/shard_map/all_gather | solution.py:85
  8.6 26.8 %copy-start.21 = (bf16[2,384,2,64]{1,3,2,0:T(8,128)(2,1)S(1)}, bf16[2,384,2,64]{1,3,2,0:T(8,128)(2,1)}, u32[]{:S(2)}) copy-start(bf16[2,384,2,64]{1,3,2,0:T(8,128)(2,1)} %param.23) | copy-start | bytes 589828
  8.6 84.7 %all-gather.30.cloned.1.call-start = ((), (), s32[]{:S(2)}) async-start(), calls=%async_computation.4 | async-start | bytes 3932160 | tf_op jit(solution)/shard_map/all_gather | solution.py:92
  13.7 125.8 %all-gather.40.cloned.1.call-start = ((), (), s32[]{:S(2)}) async-start(), calls=%async_computation.13 | async-start | bytes 1474560 | tf_op jit(solution)/shard_map/all_gather | solution.py:88
  14.7 240.2 %reduce-scatter.5.cloned.1.call-start = ((), (), s32[]{:S(2)}) async-start(), calls=%async_computation.5 | async-start | bytes 7864320 | tf_op jit(solution)/shard_map/reduce_scatter | solution.py:100
  43.1 64.2 %copy-start.8 = (f32[1024,32]{0,1:T(8,128)}, f32[1024,32]{0,1:T(8,128)S(1)}, u32[]{:S(2)}) copy-start(f32[1024,32]{0,1:T(8,128)S(1)} %get-tuple-element.236) | copy-start | bytes 393220
  43.1 64.2 %copy-start.10 = (f32[1024,32]{0,1:T(8,128)}, f32[1024,32]{0,1:T(8,128)S(1)}, u32[]{:S(2)}) copy-start(f32[1024,32]{0,1:T(8,128)S(1)} %get-tuple-element.237) | copy-start | bytes 393220
  96.9 8.2 copy-start
  105.1 2.3 copy-start.12
  107.4 1.2 copy-start.13
  145.3 109.6 %copy-start.2 = (bf16[256,1536]{1,0:T(8,128)(2,1)S(1)}, bf16[256,1536]{1,0:T(8,128)(2,1)}, u32[]{:S(2)}) copy-start(bf16[256,1536]{1,0:T(8,128)(2,1)} %param.17) | copy-start | bytes 2359300
  145.3 194.3 %all-gather.32.cloned.1.call-start = ((), (), s32[]{:S(2)}) async-start(), calls=%async_computation.6 | async-start | bytes 3932160 | tf_op jit(solution)/shard_map/all_gather | solution.py:101
  254.9 1.9 copy-start.5
  258.0 167.6 %all-gather.42.cloned.1.call-start = ((), (), s32[]{:S(2)}) async-start(), calls=%async_computation.14 | async-start | bytes 19660800 | tf_op jit(solution)/shard_map/all_gather | solution.py:89
  263.8 264.2 %all-gather.44.cloned.1.call-start = ((), (), s32[]{:S(2)}) async-start(), calls=%async_computation.15 | async-start | bytes 19660800 | tf_op jit(solution)/shard_map/all_gather | solution.py:90
  269.6 360.7 %all-gather.46.cloned.1.call-start = ((), (), s32[]{:S(2)}) async-start(), calls=%async_computation.16 | async-start | bytes 19660800 | tf_op jit(solution)/shard_map/all_gather | solution.py:91
  275.6 33.3 %copy-start.31 = (f32[256,2]{0,1:T(2,128)S(1)}, f32[256,2]{0,1:T(2,128)}, u32[]{:S(2)}) copy-start(f32[256,2]{0,1:T(2,128)} %param.20) | copy-start | bytes 6148
  275.6 530.3 %reduce-scatter.7.cloned.1.call-start = ((), (), s32[]{:S(2)}) async-start(), calls=%async_computation.7 | async-start | bytes 7864320 | tf_op jit(solution)/shard_map/reduce_scatter | solution.py:103
  327.8 11.9 copy-start.24
  327.8 340.4 %copy-start.29 = (s32[2048]{0:T(1024)}, s32[2048]{0:T(1024)S(1)}, u32[]{:S(2)}) copy-start(s32[2048]{0:T(1024)S(1)} %get-tuple-element.235) | copy-start | bytes 24580
  339.6 328.6 %copy-start.22 = (f32[2048]{0:T(1024)}, f32[2048]{0:T(1024)S(1)}, u32[]{:S(2)}) copy-start(f32[2048]{0:T(1024)S(1)} %gather_fusion.1) | copy-start | bytes 24580
  528.0 36.4 %copy-start.6 = (f32[2048,128]{1,0:T(8,128)S(1)}, f32[2048,128]{1,0:T(8,128)}, u32[]{:S(2)}) copy-start(f32[2048,128]{1,0:T(8,128)} %ragged-dot-none.5) | copy-start | bytes 3145732
  694.0 114.9 %copy-start.26 = (f32[1536]{0:T(1024)S(1)}, f32[1536]{0:T(1024)}, u32[]{:S(2)}) copy-start(f32[1536]{0:T(1024)} %get-tuple-element.165) | copy-start | bytes 18436
  694.0 179.6 %all-gather.34.cloned.1.call-start = ((), (), s32[]{:S(2)}) async-start(), calls=%async_computation.8 | async-start | bytes 3932160 | tf_op jit(solution)/shard_map/all_gather | solution.py:92
  807.7 3.6 copy-start.18
  807.7 10.1 copy-start.19
  810.0 81.3 %all-gather.48.cloned.1.call-start = ((), (), s32[]{:S(2)}) async-start(), calls=%async_computation.17 | async-start | bytes 1474560 | tf_op jit(solution)/shard_map/all_gather | solution.py:85
  810.7 121.1 %all-gather.50.cloned.1.call-start = ((), (), s32[]{:S(2)}) async-start(), calls=%async_computation.18 | async-start | bytes 1474560 | tf_op jit(solution)/shard_map/all_gather | solution.py:88
  811.3 237.0 %reduce-scatter.9.cloned.1.call-start = ((), (), s32[]{:S(2)}) async-start(), calls=%async_computation.9 | async-start | bytes 7864320 | tf_op jit(solution)/shard_map/reduce_scatter | solution.py:100
  817.8 59.0 %copy-start.9 = (f32[1024,32]{0,1:T(8,128)S(1)}, f32[1024,32]{0,1:T(8,128)}, u32[]{:S(2)}) copy-start(f32[1024,32]{0,1:T(8,128)} %copy-done.8) | copy-start | bytes 393220
  817.8 59.1 %copy-start.11 = (f32[1024,32]{0,1:T(8,128)S(1)}, f32[1024,32]{0,1:T(8,128)}, u32[]{:S(2)}) copy-start(f32[1024,32]{0,1:T(8,128)} %copy-done.10) | copy-start | bytes 393220
  873.6 17.7 %copy-start.1 = (bf16[1024,1536]{1,0:T(8,128)(2,1)S(1)}, bf16[1024,1536]{1,0:T(8,128)(2,1)}, u32[]{:S(2)}) copy-start(bf16[1024,1536]{1,0:T(8,128)(2,1)} %all-gather.34.cloned.1.call-done) | copy-start | bytes 9437188
  898.6 2.3 copy-start.16
  898.6 2.3 copy-start.17
  898.6 2.3 copy-start.14
  937.6 110.7 %copy-start.4 = (f32[256,1536]{1,0:T(8,128)S(1)}, f32[256,1536]{1,0:T(8,128)}, u32[]{:S(2)}) copy-start(f32[256,1536]{1,0:T(8,128)} %copy-done.3) | copy-start | bytes 4718596
  937.6 112.4 %copy-start.27 = (f32[1536]{0:T(1024)S(1)}, f32[1536]{0:T(1024)}, u32[]{:S(2)}) copy-start(f32[1536]{0:T(1024)} %get-tuple-element.163) | copy-start | bytes 18436
  937.6 177.1 %all-gather.36.cloned.1.call-start = ((), (), s32[]{:S(2)}) async-start(), calls=%async_computation.10 | async-start | bytes 3932160 | tf_op jit(solution)/shard_map/all_gather | solution.py:101
  1051.1 164.8 %all-gather.52.cloned.1.call-start = ((), (), s32[]{:S(2)}) async-start(), calls=%async_computation.19 | async-start | bytes 19660800 | tf_op jit(solution)/shard_map/all_gather | solution.py:89
  1051.7 266.6 %all-gather.54.cloned.1.call-start = ((), (), s32[]{:S(2)}) async-start(), calls=%async_computation.20 | async-start | bytes 19660800 | tf_op jit(solution)/shard_map/all_gather | solution.py:90
  1051.7 63.0 %copy-start.25 = (s32[2048]{0:T(1024)S(1)}, s32[2048]{0:T(1024)}, u32[]{:S(2)}) copy-start(s32[2048]{0:T(1024)} %copy-done.24) | copy-start | bytes 24580
  1052.3 368.2 %all-gather.56.cloned.1.call-start = ((), (), s32[]{:S(2)}) async-start(), calls=%async_computation.21 | async-start | bytes 19660800 | tf_op jit(solution)/shard_map/all_gather | solution.py:91
  1052.9 543.2 %reduce-scatter.11.cloned.1.call-start = ((), (), s32[]{:S(2)}) async-start(), calls=%async_computation.11 | async-start | bytes 7864320 | tf_op jit(solution)/shard_map/reduce_scatter | solution.py:103
  1318.3 36.4 %copy-start.7 = (f32[2048,128]{1,0:T(8,128)S(1)}, f32[2048,128]{1,0:T(8,128)}, u32[]{:S(2)}) copy-start(f32[2048,128]{1,0:T(8,128)} %ragged-dot-none.2) | copy-start | bytes 3145732
  1420.4 37.9 %copy-start.23 = (f32[2048]{0:T(1024)S(1)}, f32[2048]{0:T(1024)}, u32[]{:S(2)}) copy-start(f32[2048]{0:T(1024)} %copy-done.22) | copy-start | bytes 24580
  (3 other events, 2.5 us)
Sparse Core Ops, SparseCore 0:
  8.9 19.9 all-gather.37
  30.5 62.7 all-gather.29
  94.8 16.0 all-gather.39
  145.4 109.3 reduce-scatter.4
  258.1 64.8 all-gather.31
  324.4 101.0 all-gather.41
  427.1 100.8 all-gather.43
  529.6 100.6 all-gather.45
  694.1 111.7 reduce-scatter.6
  810.1 63.4 all-gather.33
  875.2 16.0 all-gather.47
  892.7 17.2 all-gather.49
  937.7 110.5 reduce-scatter.8
  1051.2 63.4 all-gather.35
  1116.1 99.7 all-gather.51
  1217.4 100.9 all-gather.53
  1319.7 100.6 all-gather.55
  1484.2 111.7 reduce-scatter.10
where the time goes:
time: 1620 us; the launch traced here: 1610 us
  waiting for transfers between devices  1040 us (64%)
  Pallas kernels  224 us (14%)
  other arithmetic  100 us (6%)
  matrix products  82.8 us (5%)
  local copies, waits for them, and re-layouts  82.1 us (5%)
  blocking collectives  66 us (4%)
    reduce_scatter x2, waiting for transfers between devices, device_step(): lax.psum_scatter(mix_part, 'mp', scatter_dimension=0, tiled=True)  224 us
    another operation x6, Pallas kernels  221 us
    reduce_scatter x2, waiting for transfers between devices, device_step(): lax.psum_scatter(attn_part, 'mp', scatter_dimension=0, tiled=True)  219 us
    all_gather x2, waiting for transfers between devices, device_step(): gate_weight = lax.all_gather(w_gate[layer], 'tok', axis=1, tiled=True)  156 us
    all_gather x2, waiting for transfers between devices, device_step(): up_weight = lax.all_gather(w_up[layer], 'tok', axis=1, tiled=True)  132 us
    all_gather x2, waiting for transfers between devices, device_step(): down_weight = lax.all_gather(w_down[layer], 'tok', axis=2, tiled=True)  127 us
    all_gather x2, waiting for transfers between devices, device_step(): lax.all_gather(rms_norm(residual, gain_attn[layer]), 'mp', axis=0, tiled=...  99.1 us
    all_gather x2, waiting for transfers between devices, device_step(): lax.all_gather(rms_norm(residual, gain_mlp[layer]), 'mp', axis=0, tiled=T...  61.6 us
  transfers between devices with their start and end apart: 18, of which 14 were waited for; matrix products, arithmetic and copies ran while one was open for 12% of the time, Pallas kernels for 9%

commit v1 on v0

v1 whole, which is shorter than its diff:
```python
import jax
import jax.numpy as jnp
from jax import lax
from jax.experimental import pallas as pl
from jax.experimental.pallas import tpu as pltpu
from jax.sharding import PartitionSpec as P


EPS = 1e-5
ROPE_BASE = 10000.0
ROW_ALIGN = 16
ROW_BLOCK = 64
GATHER_ROWS = 256


def rms_norm(residual, gain):
    inv_rms = lax.rsqrt(jnp.mean(residual * residual, axis=-1, keepdims=True) + EPS)
    return (residual * inv_rms * gain.astype(jnp.float32)).astype(jnp.bfloat16)


def request_positions(seg_rows):
    token_index = jnp.arange(seg_rows.shape[-1], dtype=jnp.int32)
    is_start = jnp.concatenate([jnp.ones(seg_rows.shape[:-1] + (1,), dtype=jnp.bool_), seg_rows[..., 1:] != seg_rows[..., :-1]], axis=-1)
    start_index = lax.cummax(jnp.where(is_start, token_index, 0), axis=seg_rows.ndim - 1)
    return token_index - start_index


def rope_tables(positions, head_dim):
    inv_freq = jnp.power(ROPE_BASE, -jnp.arange(head_dim // 2, dtype=jnp.float32) * 2.0 / head_dim)
    angles = positions.astype(jnp.float32)[..., None] * inv_freq
    return jnp.cos(angles)[..., None, :], jnp.sin(angles)[..., None, :]


def apply_rope(vectors, cosines, sines):
    half_dim = vectors.shape[-1] // 2
    first_half = vectors[..., :half_dim]
    second_half = vectors[..., half_dim:]
    return jnp.concatenate([first_half * cosines - second_half * sines, second_half * cosines + first_half * sines], axis=-1)


def block_attention(q_rot, k_rot, v_all, seg_query, query_index, seg_keys, key_index):
    n_query, kv_heads, groups, head_dim = q_rot.shape
    block = min(n_query, 512)
    num_blocks = n_query // block
    scale = head_dim ** -0.5

    def one_block(block_in):
        q_block, seg_block, index_block = block_in
        scores = jnp.einsum('bhgd,shd->hgbs', q_block, k_rot, preferred_element_type=jnp.float32) * scale
        allowed = (seg_block[:, None] == seg_keys[None, :]) & (key_index[None, :] <= index_block[:, None])
        attn_prob = jax.nn.softmax(jnp.where(allowed, scores, -1e30), axis=-1).astype(jnp.bfloat16)
        return jnp.einsum('hgbs,shd->bhgd', attn_prob, v_all, preferred_element_type=jnp.float32).astype(jnp.bfloat16)

    block_outs = lax.map(one_block, (q_rot.reshape(num_blocks, block, kv_heads, groups, head_dim), seg_query.reshape(num_blocks, block), query_index.reshape(num_blocks, block)))
    return block_outs.reshape(n_query, kv_heads * groups, head_dim)


def moe_kernel(place_ref, start_ref, count_ref, pos_ref, gate_ref, pos0_ref, pos1_ref, h_ref, *rest):
    weights, (out_ref, x_ref, d_ref) = rest[:24], rest[24:]
    step = pl.program_id(0)
    my_slice = place_ref[1]
    parts, slices, part_rows, width = h_ref.shape
    rows = x_ref.shape[1]

    @pl.when(step == 0)
    def _():
        def gather_rows(chunk, carry):
            base = pl.multiple_of(chunk * GATHER_ROWS, GATHER_ROWS)
            row_ids = base + lax.broadcasted_iota(jnp.int32, (GATHER_ROWS, part_rows), 0)
            picks = [((pos0_ref[part] == row_ids) | (pos1_ref[part] == row_ids)).astype(jnp.float32).astype(jnp.bfloat16) for part in range(parts)]
            for k in range(slices):
                acc = jnp.zeros((GATHER_ROWS, width), jnp.float32)
                for part in range(parts):
                    acc += jnp.dot(picks[part], h_ref[part, my_slice ^ k], preferred_element_type=jnp.float32)
                x_ref[k, pl.ds(base, GATHER_ROWS), :] = acc.astype(jnp.bfloat16)
            return carry

        lax.fori_loop(0, rows // GATHER_ROWS, gather_rows, 0)

    def one_expert(rank, gate_w, up_w, down_w):
        start = start_ref[rank]

        def one_block(block, carry):
            base = pl.multiple_of(start + block * ROW_BLOCK, ROW_ALIGN)
            gate_pre = jnp.zeros((ROW_BLOCK, gate_w[0].shape[1]), jnp.float32)
            up_pre = jnp.zeros((ROW_BLOCK, gate_w[0].shape[1]), jnp.float32)
            for k in range(slices):
                x_rows = x_ref[k, pl.ds(base, ROW_BLOCK), :]
                gate_pre += jnp.dot(x_rows, gate_w[k][...], preferred_element_type=jnp.float32)
                up_pre += jnp.dot(x_rows, up_w[k][...], preferred_element_type=jnp.float32)
            act = (jax.nn.silu(gate_pre) * up_pre).astype(jnp.bfloat16)
            for k in range(slices):
                d_ref[k, pl.ds(base, ROW_BLOCK), :] = jnp.dot(act, down_w[k][...], preferred_element_type=jnp.float32)
            return carry

        lax.fori_loop(0, count_ref[rank], one_block, 0)

    own_half, other_half = [0, 2, 4, 6], [1, 3, 5, 7]
    for half, order in enumerate((own_half, other_half)):
        one_expert(2 * step + half, [weights[j] for j in order], [weights[8 + j] for j in order], [weights[16 + j] for j in order])

    @pl.when(step == pl.num_programs(0) - 1)
    def _():
        for part in range(parts):
            def mix_rows(group, carry):
                base = pl.multiple_of(group * 8, 8)
                for u in range(8):
                    pair = 2 * (part * part_rows + base + u)
                    p0, p1 = pos_ref[pair], pos_ref[pair + 1]
                    g0, g1 = gate_ref[pair], gate_ref[pair + 1]
                    for k in range(slices):
                        out_ref[part * slices + (my_slice ^ k), pl.ds(base + u, 1), :] = d_ref[k, pl.ds(p0, 1), :] * g0 + d_ref[k, pl.ds(p1, 1), :] * g1
                return carry

            lax.fori_loop(0, part_rows // 8, mix_rows, 0)


def expert_mix(layer, place, route, h_all, weight_sets):
    starts, blocks, pair_pos, pair_gate, pos0, pos1, rows = route
    parts, slices, part_rows, width = h_all.shape
    half = weight_sets[0][2].shape[0]

    def whole(ndim):
        return lambda i, *_: (0,) * ndim

    in_specs = [pl.BlockSpec(memory_space=pltpu.SMEM), pl.BlockSpec(pos0.shape, whole(3)), pl.BlockSpec(pos1.shape, whole(3)), pl.BlockSpec(h_all.shape, whole(4))]
    operands = [pair_gate, pos0, pos1, h_all]
    for own, peer, y_half, x_half, y_far, x_far in weight_sets:
        block = own.shape[2:]
        near = pl.BlockSpec((None, None) + block, lambda i, place, *_: (layer, half * place[0] + i, 0, 0))
        far = pl.BlockSpec((None, None) + block, lambda i, place, *_: (layer, half * (1 - place[0]) + i, 0, 0))
        piece = pl.BlockSpec((None,) + block, lambda i, *_: (i, 0, 0))
        in_specs += [near, far, near, far, piece, piece, piece, piece]
        operands += [own, own, peer, peer, y_half, x_half, y_far, x_far]
    flops = 2 * rows * parts * part_rows * slices * width + 6 * 2 * parts * part_rows * slices * width * 128
    return pl.pallas_call(
        moe_kernel,
        grid_spec=pltpu.PrefetchScalarGridSpec(
            num_scalar_prefetch=4,
            grid=(half,),
            in_specs=in_specs,
            out_specs=pl.BlockSpec((parts * slices, part_rows, width), whole(3)),
            scratch_shapes=[pltpu.VMEM((slices, rows, width), jnp.bfloat16), pltpu.VMEM((slices, rows, width), jnp.float32)],
        ),
        out_shape=jax.ShapeDtypeStruct((parts * slices, part_rows, width), jnp.float32),
        compiler_params=pltpu.CompilerParams(vmem_limit_bytes=60 * 1024 * 1024, dimension_semantics=("arbitrary",)),
        cost_estimate=pl.CostEstimate(flops=flops * 4, bytes_accessed=60_000_000, transcendentals=0),
        name="expert_mix",
    )(place, starts, blocks, pair_pos, *operands)


def routing(ids, gates, num_experts, my_rep, parts, part_rows):
    half = num_experts // 2
    pairs = ids.shape[0]
    rank = 2 * (ids % half) + (ids // half != my_rep).astype(jnp.int32)
    hits = (rank[:, None] == jnp.arange(num_experts, dtype=jnp.int32)[None, :])
    index = jnp.arange(pairs, dtype=jnp.int32)
    before = (index[:, None] > index[None, :]).astype(jnp.bfloat16)
    place_in = jnp.dot(before, hits.astype(jnp.bfloat16), preferred_element_type=jnp.float32)
    counts = jnp.sum(hits.astype(jnp.int32), axis=0)
    padded = (counts + (ROW_ALIGN - 1)) // ROW_ALIGN * ROW_ALIGN
    order = jnp.arange(num_experts, dtype=jnp.int32)
    starts = jnp.sum(jnp.where(order[None, :] < order[:, None], padded[None, :], 0), axis=1)
    blocks = (counts + (ROW_BLOCK - 1)) // ROW_BLOCK
    pair_pos = jnp.sum(jnp.where(hits, place_in.astype(jnp.int32) + starts[None, :], 0), axis=1)
    two = pair_pos.reshape(parts, part_rows, 2)
    rows = pairs + num_experts * (ROW_ALIGN - 1) + ROW_BLOCK
    rows = (rows + GATHER_ROWS - 1) // GATHER_ROWS * GATHER_ROWS
    return starts, blocks, pair_pos, gates.reshape(pairs), two[:, None, :, 0], two[:, None, :, 1], rows


def solution(mesh):
    n_tok, n_mp = mesh.shape['tok'], mesh.shape['mp']
    token_spec = P(('rep', 'tok', 'mp'))
    row_spec = P(('rep', 'tok', 'mp'), None)
    head_weight = P(None, 'tok', 'mp', None)
    in_specs = (row_spec, token_spec, row_spec, row_spec, head_weight, head_weight, head_weight, P(None, 'mp', None, 'tok'), P(None, None, 'tok', 'mp'), P(None, None, 'tok', 'mp'), P(None, None, 'mp', 'tok'), P(None, None), P(None, None))
    swap_perm = [(m * n_tok + t, t * n_tok + m) for t in range(n_tok) for m in range(n_mp)]
    core_perm = [(t, t ^ 1) for t in range(n_tok)]
    y_perm = [(t, t ^ 2) for t in range(n_tok)]
    x_perm = [(0, 1), (1, 0)]

    def swap_roles(value):
        return lax.ppermute(value, ('mp', 'tok'), swap_perm)

    def device_step(hidden_in, seg_ids, expert_ids, expert_gates, w_query, w_key, w_value, w_out, w_gate, w_up, w_down, gain_attn, gain_mlp):
        num_layers, slice_width, q_local, head_dim = w_query.shape
        kv_local = w_key.shape[2]
        groups = q_local // kv_local
        num_experts = w_gate.shape[1]
        half = num_experts // 2
        part_rows = hidden_in.shape[0]
        my_rep, my_tok, my_mp = lax.axis_index('rep'), lax.axis_index('tok'), lax.axis_index('mp')
        place = jnp.stack([my_rep, my_tok]).astype(jnp.int32)
        hidden_width = slice_width * n_tok
        attn_cols = (q_local + 2 * kv_local) * head_dim

        swapped = swap_roles(hidden_in)
        residual = swapped.astype(jnp.float32)
        attn_packs = []
        for layer in range(num_layers):
            qkv = jnp.concatenate([w_query[layer], w_key[layer], w_value[layer]], axis=1).reshape(slice_width, attn_cols)
            pack = jnp.concatenate([qkv, w_out[layer].reshape(q_local * head_dim, slice_width)], axis=1)
            attn_packs.append(swap_roles(pack))

        expert_weights = (w_gate, w_up, w_down)
        peers = []
        for own in expert_weights:
            peers.append(lax.ppermute(own, 'tok', core_perm))
        layer_sets = []
        for layer in range(num_layers):
            sets = []
            for own, peer in zip(expert_weights, peers):
                mine = lax.dynamic_slice(own, (layer, my_rep * half, 0, 0), (1, half) + own.shape[2:])[0]
                y_half = lax.ppermute(mine, 'tok', y_perm)
                x_half = lax.ppermute(y_half, 'rep', x_perm)
                y_far = lax.ppermute(y_half, 'tok', core_perm)
                x_far = lax.ppermute(x_half, 'tok', core_perm)
                sets.append((own, peer, y_half, x_half, y_far, x_far))
            layer_sets.append(sets)

        seg_all = lax.all_gather(seg_ids, ('tok', 'mp'), axis=0)
        pair_info = jnp.concatenate([expert_ids.astype(jnp.float32), expert_gates], axis=1)
        pair_all = lax.all_gather(pair_info, ('tok', 'mp'), axis=0).reshape(n_tok, n_mp, part_rows, 4)
        seg_full = lax.dynamic_index_in_dim(seg_all.reshape(n_tok, n_mp * part_rows), my_mp, axis=0, keepdims=False)
        pair_mine = lax.dynamic_index_in_dim(pair_all, my_tok, axis=1, keepdims=False).reshape(n_tok * part_rows, 4)
        route = routing(pair_mine[:, :2].astype(jnp.int32).reshape(-1), pair_mine[:, 2:], num_experts, my_rep, n_tok, part_rows)
        seq_len = seg_full.shape[0]
        token_index = jnp.arange(seq_len, dtype=jnp.int32)
        cosines, sines = rope_tables(request_positions(seg_full), head_dim)
        for layer in range(num_layers):
            pack = lax.all_gather(attn_packs[layer], 'mp', axis=0)
            qkv_weight = pack[:, :, :attn_cols].reshape(hidden_width, attn_cols)
            o_weight = pack[:, :, attn_cols:]
            normed = rms_norm(residual, gain_attn[layer])
            normed = lax.all_gather(normed, 'tok', axis=0, tiled=True)
            qkv = jnp.dot(normed, qkv_weight, preferred_element_type=jnp.float32)
            qkv = qkv.reshape(seq_len, q_local + 2 * kv_local, head_dim)
            rotated = apply_rope(qkv[:, :q_local + kv_local], cosines, sines).astype(jnp.bfloat16)
            q_rot = rotated[:, :q_local].reshape(seq_len, kv_local, groups, head_dim)
            k_rot = rotated[:, q_local:]
            v_all = qkv[:, q_local + kv_local:].astype(jnp.bfloat16)
            attn_out = block_attention(q_rot, k_rot, v_all, seg_full, token_index, seg_full, token_index)
            attn_part = jnp.einsum('sk,tkw->stw', attn_out.reshape(seq_len, q_local * head_dim), o_weight, preferred_element_type=jnp.float32)
            attn_part = attn_part.reshape(seq_len, hidden_width)
            residual = residual + lax.psum_scatter(attn_part, 'tok', scatter_dimension=0, tiled=True)
            normed = rms_norm(residual, gain_mlp[layer])
            normed = normed.reshape(part_rows, n_tok, slice_width).transpose(1, 0, 2)
            h_all = lax.all_gather(normed, 'mp', axis=0)
            mix_part = expert_mix(layer, place, route, h_all, layer_sets[layer])
            mix = lax.psum_scatter(mix_part, 'mp', scatter_dimension=0, tiled=True)
            residual = residual + mix.transpose(1, 0, 2).reshape(part_rows, hidden_width)
        return swap_roles(residual)

    return jax.shard_map(device_step, mesh=mesh, in_specs=in_specs, out_specs=row_spec, check_vma=False)
```

time: 1620 us -> 1360 us (0.84)
  the two profiles are of different devices: /device:TPU:0 before, /device:TPU:4 now
where the time goes in v1:
time: 1360 us
  waiting for transfers between devices  925 us (68%)
  Pallas kernels  118 us (9%)
  matrix products  91.6 us (7%)
  local copies, waits for them, and re-layouts  84.9 us (6%)
  blocking collectives  68.7 us (5%)
  starting transfers between devices  33.8 us (2%)
  other arithmetic  20.4 us (1%)
  between operations  14.5 us (1%)
    ppermute x4, waiting for transfers between devices, swap_roles(): return lax.ppermute(value, ('mp', 'tok'), swap_perm)  269 us
    ppermute x6, waiting for transfers between devices, device_step(): y_half = lax.ppermute(mine, 'tok', y_perm)  210 us
    reduce_scatter x2, waiting for transfers between devices, device_step(): mix = lax.psum_scatter(mix_part, 'mp', scatter_dimension=0, tiled=True)  148 us
    pallas_call x2, Pallas kernels, expert_mix(): pl.pallas_call(moe_kernel, grid_spec=pltpu.PrefetchScalarGridSpec(num_sca...  118 us
    ppermute x6, waiting for transfers between devices, device_step(): x_half = lax.ppermute(y_half, 'rep', x_perm)  98.2 us
    reduce_scatter x2, waiting for transfers between devices, device_step(): lax.psum_scatter(attn_part, 'tok', scatter_dimension=0, tiled=True)  88.9 us
    all_gather x2, waiting for transfers between devices, device_step(): pack = lax.all_gather(attn_packs[layer], 'mp', axis=0)  73.7 us
    sub x4, matrix products, one_block(): jax.nn.softmax(jnp.where(allowed, scores, -1e+30), axis=-1)  40.8 us
  transfers between devices with their start and end apart: 41, of which 22 were waited for; matrix products, arithmetic and copies ran while one was open for 5% of the time, Pallas kernels for 0%

profile of v1, /device:TPU:4, one launch (start us, length us, event | category | flops | bytes accessed | tf_op | source)
XLA Modules:
  0.0 1356.4 jit_solution(3626027823573227337)
XLA Ops:
  11.7 4.4 collective-permute-start.1
  16.1 44.5 %collective-permute-done.1 = bf16[384,1024]{0,1:T(8,128)(2,1)S(1)} collective-permute-done((bf16[384,1024]{0,1:T(8,128)(2,1)S(1)}, bf16[384,1024]{0,1:T(8,128)(2,1)S(1)}, u32[]{:S(2)}, u32[]{:S(2)}) %collective-permute-start.1) | collective-permute-done | bytes 786464 | tf_op jit(solution)/shard_map/ppermute | solution.py:184
  64.1 69.8 %collective-permute-done = bf16[256,1536]{1,0:T(8,128)(2,1)S(1)} collective-permute-done((bf16[256,1536]{1,0:T(8,128)(2,1)S(1)}, bf16[256,1536]{1,0:T(8,128)(2,1)S(1)}, u32[]{:S(2)}, u32[]{:S(2)}) %collective-permute-start) | collective-permute-done | bytes 786464 | tf_op jit(solution)/shard_map/ppermute | solution.py:184
  135.5 30.7 %all-gather.6 = s32[16,1,256]{2,1,0:T(1,128)S(1)} all-gather(s32[1,1,256]{2,1,0:T(1,128)S(1)} %bitcast.273), channel_id=2, replica_groups=mesh['rep'=2,'mp'=4,'tok'=4] {'tok','mp'}, dimensions={0}, use_global_device_ids=true | all-gather | bytes 17408 | tf_op jit(solution)/shard_map/all_gather | solution.py:222
  168.9 5.3 copy.118
  178.3 4.7 fusion.81
  189.5 35.7 %while.22 = (s32[]{:T(128)}, bf16[2,512,2,3,64]{1,4,3,2,0:T(8,128)(2,1)}, s32[2,512]{1,0:T(2,128)S(1)}, s32[1024]{0:T(1024)S(1)}, s32[2,512]{1,0:T(2,128)S(1)}, ...) while((s32[]{:T(128)}, ...), condition=%wide.region_6.7_spmd.clone, body=%wide.region_3.6_spmd.clone.sunk | while | flops 825951232 | bytes 27567200 | solution.py:54
  190.1 9.8 fusion.147
  199.9 7.4 fusion.148
  207.9 9.8 fusion.147
  217.8 7.4 fusion.148
  229.1 5.6 fusion.123
  234.8 3.9 dynamic-slice_bitcast_fusion.1
  238.7 4.4 dynamic-slice_bitcast_fusion
  245.2 4.1 dynamic-slice_bitcast_fusion.2
  249.4 64.0 %collective-permute-done.8.rest_12_ = bf16[20,384,128]{2,1,0:T(8,128)(2,1)S(1)} collective-permute-done((bf16[20,384,128]{2,1,0:T(8,128)(2,1)S(1)}, bf16[20,384,128]{2,1,0:T(8,128)(2,1)S(1)}, u32[]{:S(2)}, u32[]{:S(2)}) %collective-permute-start.8) | collective-permute-done | bytes 1966112 | tf_op jit(solution)/shard_map/ppermute | solution.py:215
  314.7 45.6 %collective-permute-done.13.rest_20_ = bf16[20,128,384]{2,1,0:T(8,128)(2,1)} collective-permute-done((bf16[20,128,384]{2,1,0:T(8,128)(2,1)S(1)}, bf16[20,128,384]{2,1,0:T(8,128)(2,1)}, u32[]{:S(2)}, u32[]{:S(2)}) %collective-permute-start.13) | collective-permute-done | bytes 1966112 | tf_op jit(solution)/shard_map/ppermute | solution.py:215
  361.8 36.6 %collective-permute-done.3.rest_4_ = bf16[20,384,128]{2,1,0:T(8,128)(2,1)S(1)} collective-permute-done((bf16[20,384,128]{2,1,0:T(8,128)(2,1)S(1)}, bf16[20,384,128]{2,1,0:T(8,128)(2,1)S(1)}, u32[]{:S(2)}, u32[]{:S(2)}) %collective-permute-start.3) | collective-permute-done | bytes 1966112 | tf_op jit(solution)/shard_map/ppermute | solution.py:215
  400.9 38.7 %collective-permute-done.4.rest_5_ = bf16[20,384,128]{2,1,0:T(8,128)(2,1)S(1)} collective-permute-done((bf16[20,384,128]{2,1,0:T(8,128)(2,1)S(1)}, bf16[20,384,128]{2,1,0:T(8,128)(2,1)S(1)}, u32[]{:S(2)}, u32[]{:S(2)}) %collective-permute-start.4) | collective-permute-done | bytes 1966112 | tf_op jit(solution)/shard_map/ppermute | solution.py:216
  445.4 3.7 collective-permute-done.5.rest_6_
  453.3 38.0 %all-gather.2 = f32[4096,4]{0,1:T(4,128)S(1)} all-gather(f32[256,4]{0,1:T(4,128)S(1)} %pad_maximum_fusion.6), channel_id=4, replica_groups=mesh['rep'=2,'mp'=4,'tok'=4] {'tok','mp'}, dimensions={0}, use_global_device_ids=true | all-gather | bytes 69632 | tf_op jit(solution)/shard_map/all_gather | solution.py:224
  499.3 13.5 all-gather.20.cloned.1.call-done
  512.8 58.9 %expert_mix.2 = f32[16,256,384]{2,1,0:T(8,128)} custom-call(s32[2]{0:T(128)} %pad_add_fusion.place_ref, s32[40]{0:T(128)} %copy-done.37, s32[40]{0:T(128)} %get-tuple-element.323.count_ref, s32[2048]{0:T(1024)} %copy-done.17, f32[2048]{0:T(1024)} %reshape.262.gate_ref, s32[4,1,256]{2,1,0:T(1,128)} %bitcast.269, s32[4,1,256]{2,1,0:T(1,128)} %bitcast.271, ...), custom_call_target="tpu_custom_call" | custom-call | flops 45097156608 | bytes 60000000 | tf_op jit(solution)/shard_map/expert_mix/pallas_call | solution.py:136
  572.9 3.7 collective-permute-start.17
  576.7 85.1 %collective-permute-done.17 = bf16[384,1024]{0,1:T(8,128)(2,1)S(1)} collective-permute-done((bf16[384,1024]{0,1:T(8,128)(2,1)S(1)}, bf16[384,1024]{0,1:T(8,128)(2,1)S(1)}, u32[]{:S(2)}, u32[]{:S(2)}) %collective-permute-start.17) | collective-permute-done | bytes 786464 | tf_op jit(solution)/shard_map/ppermute | solution.py:184
  662.9 35.0 %reduce-scatter.7.cloned.1.call-done = f32[4,256,384]{2,1,0:T(8,128)} async-done(((f32[16,256,384]{2,1,0:T(8,128)}), f32[4,256,384]{2,1,0:T(8,128)}) %reduce-scatter.7.cloned.1.call-update) | async-done | bytes 1572880 | tf_op jit(solution)/shard_map/reduce_scatter | solution.py:251
  704.8 73.7 %all-gather.22.cloned.1.call-done = bf16[1536,1024]{0,1:T(8,128)(2,1)} async-done(((bf16[384,1024]{0,1:T(8,128)(2,1)}), bf16[1536,1024]{0,1:T(8,128)(2,1)}) %all-gather.22.cloned.1.call-update) | async-done | bytes 3145744 | tf_op jit(solution)/shard_map/all_gather | solution.py:232
  778.5 4.7 copy.130
  786.2 4.1 copy.131
  794.5 11.6 all-gather.16.cloned.1.call-done
  806.1 4.8 fusion.79
  818.1 37.4 %while.23 = (s32[]{:T(128)}, bf16[2,512,2,3,64]{1,4,3,2,0:T(8,128)(2,1)}, s32[2,512]{1,0:T(2,128)S(1)}, s32[1024]{0:T(1024)S(1)}, s32[2,512]{1,0:T(2,128)S(1)}, ...) while((s32[]{:T(128)}, ...), condition=%wide.region_17.18_spmd.clone, body=%wide.region_14.17_spmd.clone.sunk | while | flops 825951232 | bytes 28619900 | solution.py:54
  818.7 10.6 fusion.153
  829.3 7.4 fusion.154
  837.3 10.6 fusion.153
  847.9 7.4 fusion.154
  857.7 4.5 fusion.124
  866.0 88.9 %reduce-scatter.9.cloned.1.call-done = f32[256,1536]{1,0:T(8,128)} async-done(((f32[1024,1536]{1,0:T(8,128)}), f32[256,1536]{1,0:T(8,128)}) %reduce-scatter.9.cloned.1.call-update) | async-done | bytes 1572880 | tf_op jit(solution)/shard_map/reduce_scatter | solution.py:246
  959.8 24.3 %collective-permute-done.22.rest_12_ = bf16[20,384,128]{2,1,0:T(8,128)(2,1)} collective-permute-done((bf16[20,384,128]{2,1,0:T(8,128)(2,1)}, bf16[20,384,128]{2,1,0:T(8,128)(2,1)}, u32[]{:S(2)}, u32[]{:S(2)}) %collective-permute-start.22) | collective-permute-done | bytes 1966112 | tf_op jit(solution)/shard_map/ppermute | solution.py:215
  985.8 39.7 %collective-permute-done.26.rest_20_ = bf16[20,128,384]{2,1,0:T(8,128)(2,1)} collective-permute-done((bf16[20,128,384]{2,1,0:T(8,128)(2,1)}, bf16[20,128,384]{2,1,0:T(8,128)(2,1)}, u32[]{:S(2)}, u32[]{:S(2)}) %collective-permute-start.26) | collective-permute-done | bytes 1966112 | tf_op jit(solution)/shard_map/ppermute | solution.py:215
  1027.8 18.3 %collective-permute-done.23.rest_13_ = bf16[20,384,128]{2,1,0:T(8,128)(2,1)S(1)} collective-permute-done((bf16[20,384,128]{2,1,0:T(8,128)(2,1)}, bf16[20,384,128]{2,1,0:T(8,128)(2,1)S(1)}, u32[]{:S(2)}, u32[]{:S(2)}) %collective-permute-start.23) | collective-permute-done | bytes 1966112 | tf_op jit(solution)/shard_map/ppermute | solution.py:216
  1046.1 41.1 %collective-permute-done.27.rest_21_ = bf16[20,128,384]{2,1,0:T(8,128)(2,1)S(1)} collective-permute-done((bf16[20,128,384]{2,1,0:T(8,128)(2,1)}, bf16[20,128,384]{2,1,0:T(8,128)(2,1)S(1)}, u32[]{:S(2)}, u32[]{:S(2)}) %collective-permute-start.27) | collective-permute-done | bytes 1966112 | tf_op jit(solution)/shard_map/ppermute | solution.py:216
  1087.8 3.4 collective-permute-done.25.rest_15_
  1094.2 58.8 %expert_mix.3 = f32[16,256,384]{2,1,0:T(8,128)} custom-call(s32[2]{0:T(128)} %pad_add_fusion.place_ref, s32[40]{0:T(128)} %copy-done.37, s32[40]{0:T(128)} %get-tuple-element.323.count_ref, s32[2048]{0:T(1024)} %copy-done.17, f32[2048]{0:T(1024)} %reshape.262.gate_ref, s32[4,1,256]{2,1,0:T(1,128)} %bitcast.270, s32[4,1,256]{2,1,0:T(1,128)} %bitcast.272, ...), custom_call_target="tpu_custom_call" | custom-call | flops 45097156608 | bytes 60000000 | tf_op jit(solution)/shard_map/expert_mix/pallas_call | solution.py:136
  1153.1 113.2 %reduce-scatter.11.cloned.1.call-done = f32[4,256,384]{2,1,0:T(8,128)} async-done(((f32[16,256,384]{2,1,0:T(8,128)}), f32[4,256,384]{2,1,0:T(8,128)}) %reduce-scatter.11.cloned.1.call-update) | async-done | bytes 1572880 | tf_op jit(solution)/shard_map/reduce_scatter | solution.py:251
  1269.3 3.2 copy.137
  1274.0 4.8 collective-permute-start.30
  1278.9 69.3 %collective-permute-done.30 = f32[256,1536]{1,0:T(8,128)S(1)} collective-permute-done((f32[256,1536]{1,0:T(8,128)S(1)}, f32[256,1536]{1,0:T(8,128)S(1)}, u32[]{:S(2)}, u32[]{:S(2)}) %collective-permute-start.30) | collective-permute-done | bytes 1572896 | tf_op jit(solution)/shard_map/ppermute | solution.py:184
  (247 shorter events, 102.5 us)
Async XLA Ops:
  6.5 162.4 %all-gather.18.cloned.1.call-start = ((), (), s32[]{:S(2)}) async-start(), calls=%async_computation.10 | async-start | bytes 3932160 | tf_op jit(solution)/shard_map/all_gather | solution.py:232
  10.7 50.9 %copy-start.36 = (bf16[256,1536]{1,0:T(8,128)(2,1)S(1)}, bf16[256,1536]{1,0:T(8,128)(2,1)}, u32[]{:S(2)}) copy-start(bf16[256,1536]{1,0:T(8,128)(2,1)} %param.17) | copy-start | bytes 2359300
  10.7 52.8 %copy-start.15 = (bf16[2,1536]{1,0:T(2,128)(2,1)S(1)}, bf16[2,1536]{1,0:T(2,128)(2,1)}, u32[]{:S(2)}) copy-start(bf16[2,1536]{1,0:T(2,128)(2,1)} %param.28) | copy-start | bytes 18436
  11.7 48.9 %collective-permute-start.1 = (bf16[384,1024]{0,1:T(8,128)(2,1)S(1)}, bf16[384,1024]{0,1:T(8,128)(2,1)S(1)}, u32[]{:S(2)}, u32[]{:S(2)}) collective-permute-start(bf16[384,1024]{0,1:T(8,128)(2,1)S(1)} %pad_maximum_fusion), channel_id=1, source_target_pairs={{0,0},{4,1},{8,2},{12,3},{1,4},{5,5},{9,6},{13,7},{2,8},{6,9},{10,... | collective-permute-start | bytes 2359304 | tf_op jit(solution)/shard_map/ppermute | solution.py:184
  60.6 74.8 %copy-start.20 = (s32[256]{0:T(256)S(1)}, s32[256]{0:T(256)}, u32[]{:S(2)}) copy-start(s32[256]{0:T(256)} %param.18) | copy-start | bytes 3076
  61.5 116.8 %all-gather.14.cloned.1.call-start = ((), (), s32[]{:S(2)}) async-start(), calls=%async_computation.4 | async-start | bytes 3932160 | tf_op jit(solution)/shard_map/all_gather | solution.py:236
  61.6 72.4 %collective-permute-start = (bf16[256,1536]{1,0:T(8,128)(2,1)S(1)}, bf16[256,1536]{1,0:T(8,128)(2,1)S(1)}, u32[]{:S(2)}, u32[]{:S(2)}) collective-permute-start(bf16[256,1536]{1,0:T(8,128)(2,1)S(1)} %copy-done.36), channel_id=1, source_target_pairs={{0,0},{4,1},{8,2},{12,3},{1,4},{5,5},{9,6},{13,7},{2,8},{6,9},{10,... | collective-permute-start | bytes 2359304 | tf_op jit(solution)/shard_map/ppermute | solution.py:184
  135.4 306.1 %reduce-scatter.5.cloned.1.call-start = ((), (), s32[]{:S(2)}) async-start(), calls=%async_computation.5 | async-start | bytes 7864320 | tf_op jit(solution)/shard_map/reduce_scatter | solution.py:246
  234.8 278.0 %all-gather.20.cloned.1.call-start = ((), (), s32[]{:S(2)}) async-start(), calls=%async_computation.11 | async-start | bytes 3932160 | tf_op jit(solution)/shard_map/all_gather | solution.py:249
  238.7 74.8 %collective-permute-start.8 = (bf16[20,384,128]{2,1,0:T(8,128)(2,1)S(1)}, bf16[20,384,128]{2,1,0:T(8,128)(2,1)S(1)}, u32[]{:S(2)}, u32[]{:S(2)}) collective-permute-start(bf16[20,384,128]{2,1,0:T(8,128)(2,1)S(1)} %get-tuple-element.302), channel_id=1, source_target_pairs={{0,2},{1,3},{2,0},{3,1},{4,6},{5,7},{6,4},{7,5},{8,10},{9,11},{10,... | collective-permute-start | bytes 5898248 | tf_op jit(solution)/shard_map/ppermute | solution.py:215
  243.1 197.8 %copy-start.16 = (bf16[2,1536]{1,0:T(2,128)(2,1)S(1)}, bf16[2,1536]{1,0:T(2,128)(2,1)}, u32[]{:S(2)}) copy-start(bf16[2,1536]{1,0:T(2,128)(2,1)} %param.29) | copy-start | bytes 18436
  243.1 117.2 %collective-permute-start.13 = (bf16[20,128,384]{2,1,0:T(8,128)(2,1)S(1)}, bf16[20,128,384]{2,1,0:T(8,128)(2,1)}, u32[]{:S(2)}, u32[]{:S(2)}) collective-permute-start(bf16[20,128,384]{2,1,0:T(8,128)(2,1)S(1)} %get-tuple-element.300), channel_id=1, source_target_pairs={{0,2},{1,3},{2,0},{3,1},{4,6},{5,7},{6,4},{7,5},{8,10},{9,11},{10,... | collective-permute-start | bytes 5898248 | tf_op jit(solution)/shard_map/ppermute | solution.py:215
  249.4 149.0 %collective-permute-start.3 = (bf16[20,384,128]{2,1,0:T(8,128)(2,1)S(1)}, bf16[20,384,128]{2,1,0:T(8,128)(2,1)S(1)}, u32[]{:S(2)}, u32[]{:S(2)}) collective-permute-start(bf16[20,384,128]{2,1,0:T(8,128)(2,1)S(1)} %get-tuple-element.304), channel_id=1, source_target_pairs={{0,2},{1,3},{2,0},{3,1},{4,6},{5,7},{6,4},{7,5},{8,10},{9,11},{10,... | collective-permute-start | bytes 5898248 | tf_op jit(solution)/shard_map/ppermute | solution.py:215
  313.4 130.3 %copy-start.21 = (bf16[20,384,128]{2,1,0:T(8,128)(2,1)}, bf16[20,384,128]{2,1,0:T(8,128)(2,1)S(1)}, u32[]{:S(2)}) copy-start(bf16[20,384,128]{2,1,0:T(8,128)(2,1)S(1)} %collective-permute-done.8.rest_12_) | copy-start | bytes 5898244
  313.4 87.0 %collective-permute-start.9 = (bf16[20,384,128]{2,1,0:T(8,128)(2,1)S(1)}, bf16[20,384,128]{2,1,0:T(8,128)(2,1)S(1)}, u32[]{:S(2)}, u32[]{:S(2)}) collective-permute-start(bf16[20,384,128]{2,1,0:T(8,128)(2,1)S(1)} %collective-permute-done.8.rest_12_), channel_id=1, source_target_pairs={{0,16},{16,0},{1,17},{17,1},{2,18},{18,2},{3,19},{19,3},{4,20},{20... | collective-permute-start | bytes 5898248 | tf_op jit(solution)/shard_map/ppermute | solution.py:216
  360.3 40.2 %collective-permute-start.14 = (bf16[20,128,384]{2,1,0:T(8,128)(2,1)}, bf16[20,128,384]{2,1,0:T(8,128)(2,1)S(1)}, u32[]{:S(2)}, u32[]{:S(2)}) collective-permute-start(bf16[20,128,384]{2,1,0:T(8,128)(2,1)} %collective-permute-done.13.rest_20_), channel_id=1, source_target_pairs={{0,16},{16,0},{1,17},{17,1},{2,18},{18,2},{3,19},{19,3},{4,20},{20... | collective-permute-start | bytes 5898248 | tf_op jit(solution)/shard_map/ppermute | solution.py:216
  398.4 41.2 %collective-permute-start.4 = (bf16[20,384,128]{2,1,0:T(8,128)(2,1)S(1)}, bf16[20,384,128]{2,1,0:T(8,128)(2,1)S(1)}, u32[]{:S(2)}, u32[]{:S(2)}) collective-permute-start(bf16[20,384,128]{2,1,0:T(8,128)(2,1)S(1)} %collective-permute-done.3.rest_4_), channel_id=1, source_target_pairs={{0,16},{16,0},{1,17},{17,1},{2,18},{18,2},{3,19},{19,3},{4,20},{20... | collective-permute-start | bytes 5898248 | tf_op jit(solution)/shard_map/ppermute | solution.py:216
  399.9 99.4 %collective-permute-start.12 = (bf16[2,40,128,384]{3,2,1,0:T(8,128)(2,1)}, bf16[2,40,128,384]{3,2,1,0:T(8,128)(2,1)}, u32[]{:S(2)}, u32[]{:S(2)}) collective-permute-start(bf16[2,40,128,384]{3,2,1,0:T(8,128)(2,1)} %rest_17_.3), channel_id=1, source_target_pairs={{0,1},{1,0},{2,3},{3,2},{4,5},{5,4},{6,7},{7,6},{8,9},{9,8},{10,11... | collective-permute-start | bytes 23592968 | tf_op jit(solution)/shard_map/ppermute | solution.py:209
  399.9 99.4 %collective-permute-start.2 = (bf16[2,40,384,128]{3,2,1,0:T(8,128)(2,1)}, bf16[2,40,384,128]{3,2,1,0:T(8,128)(2,1)}, u32[]{:S(2)}, u32[]{:S(2)}) collective-permute-start(bf16[2,40,384,128]{3,2,1,0:T(8,128)(2,1)} %rest_1_.3), channel_id=1, source_target_pairs={{0,1},{1,0},{2,3},{3,2},{4,5},{5,4},{6,7},{7,6},{8,9},{9,8},{10,11... | collective-permute-start | bytes 23592968 | tf_op jit(solution)/shard_map/ppermute | solution.py:209
  400.4 98.9 %collective-permute-start.7 = (bf16[2,40,384,128]{3,2,1,0:T(8,128)(2,1)}, bf16[2,40,384,128]{3,2,1,0:T(8,128)(2,1)}, u32[]{:S(2)}, u32[]{:S(2)}) collective-permute-start(bf16[2,40,384,128]{3,2,1,0:T(8,128)(2,1)} %rest_9_.3), channel_id=1, source_target_pairs={{0,1},{1,0},{2,3},{3,2},{4,5},{5,4},{6,7},{7,6},{8,9},{9,8},{10,11... | collective-permute-start | bytes 23592968 | tf_op jit(solution)/shard_map/ppermute | solution.py:209
  400.5 44.3 %collective-permute-start.10 = (bf16[20,384,128]{2,1,0:T(8,128)(2,1)S(1)}, bf16[20,384,128]{2,1,0:T(8,128)(2,1)}, u32[]{:S(2)}, u32[]{:S(2)}) collective-permute-start(bf16[20,384,128]{2,1,0:T(8,128)(2,1)S(1)} %collective-permute-done.8.rest_12_), channel_id=1, source_target_pairs={{0,1},{1,0},{2,3},{3,2},{4,5},{5,4},{6,7},{7,6},{8,9},{9,8},{10,11... | collective-permute-start | bytes 5898248 | tf_op jit(solution)/shard_map/ppermute | solution.py:217
  439.6 5.3 collective-permute-start.15
  444.7 253.2 %reduce-scatter.7.cloned.1.call-start = ((), (), s32[]{:S(2)}) async-start(), calls=%async_computation.6 | async-start | bytes 7864320 | tf_op jit(solution)/shard_map/reduce_scatter | solution.py:251
  444.8 4.2 collective-permute-start.5
  444.9 7.0 collective-permute-start.11
  449.0 50.2 %collective-permute-start.16 = (bf16[20,128,384]{2,1,0:T(8,128)(2,1)}, bf16[20,128,384]{2,1,0:T(8,128)(2,1)}, u32[]{:S(2)}, u32[]{:S(2)}) collective-permute-start(bf16[20,128,384]{2,1,0:T(8,128)(2,1)} %copy-done.24), channel_id=1, source_target_pairs={{0,1},{1,0},{2,3},{3,2},{4,5},{5,4},{6,7},{7,6},{8,9},{9,8},{10,11... | collective-permute-start | bytes 5898248 | tf_op jit(solution)/shard_map/ppermute | solution.py:218
  453.1 46.1 %collective-permute-start.6 = (bf16[20,384,128]{2,1,0:T(8,128)(2,1)}, bf16[20,384,128]{2,1,0:T(8,128)(2,1)}, u32[]{:S(2)}, u32[]{:S(2)}) collective-permute-start(bf16[20,384,128]{2,1,0:T(8,128)(2,1)} %copy-done.25), channel_id=1, source_target_pairs={{0,1},{1,0},{2,3},{3,2},{4,5},{5,4},{6,7},{7,6},{8,9},{9,8},{10,11... | collective-permute-start | bytes 5898248 | tf_op jit(solution)/shard_map/ppermute | solution.py:218
  571.7 206.8 %all-gather.22.cloned.1.call-start = ((), (), s32[]{:S(2)}) async-start(), calls=%async_computation.12 | async-start | bytes 3932160 | tf_op jit(solution)/shard_map/all_gather | solution.py:232
  572.9 88.8 %collective-permute-start.17 = (bf16[384,1024]{0,1:T(8,128)(2,1)S(1)}, bf16[384,1024]{0,1:T(8,128)(2,1)S(1)}, u32[]{:S(2)}, u32[]{:S(2)}) collective-permute-start(bf16[384,1024]{0,1:T(8,128)(2,1)S(1)} %pad_maximum_fusion.1), channel_id=1, source_target_pairs={{0,0},{4,1},{8,2},{12,3},{1,4},{5,5},{9,6},{13,7},{2,8},{6,9},{10,... | collective-permute-start | bytes 2359304 | tf_op jit(solution)/shard_map/ppermute | solution.py:184
  662.6 143.4 %all-gather.16.cloned.1.call-start = ((), (), s32[]{:S(2)}) async-start(), calls=%async_computation.7 | async-start | bytes 3932160 | tf_op jit(solution)/shard_map/all_gather | solution.py:236
  704.8 250.1 %reduce-scatter.9.cloned.1.call-start = ((), (), s32[]{:S(2)}) async-start(), calls=%async_computation.8 | async-start | bytes 7864320 | tf_op jit(solution)/shard_map/reduce_scatter | solution.py:246
  862.1 232.0 %all-gather.24.cloned.1.call-start = ((), (), s32[]{:S(2)}) async-start(), calls=%async_computation.13 | async-start | bytes 3932160 | tf_op jit(solution)/shard_map/all_gather | solution.py:249
  862.2 95.8 %collective-permute-start.18 = (bf16[20,384,128]{2,1,0:T(8,128)(2,1)}, bf16[20,384,128]{2,1,0:T(8,128)(2,1)}, u32[]{:S(2)}, u32[]{:S(2)}) collective-permute-start(bf16[20,384,128]{2,1,0:T(8,128)(2,1)} %get-tuple-element.303), channel_id=1, source_target_pairs={{0,2},{1,3},{2,0},{3,1},{4,6},{5,7},{6,4},{7,5},{8,10},{9,11},{10,... | collective-permute-start | bytes 5898248 | tf_op jit(solution)/shard_map/ppermute | solution.py:215
  863.9 120.2 %collective-permute-start.22 = (bf16[20,384,128]{2,1,0:T(8,128)(2,1)}, bf16[20,384,128]{2,1,0:T(8,128)(2,1)}, u32[]{:S(2)}, u32[]{:S(2)}) collective-permute-start(bf16[20,384,128]{2,1,0:T(8,128)(2,1)} %get-tuple-element.301), channel_id=1, source_target_pairs={{0,2},{1,3},{2,0},{3,1},{4,6},{5,7},{6,4},{7,5},{8,10},{9,11},{10,... | collective-permute-start | bytes 5898248 | tf_op jit(solution)/shard_map/ppermute | solution.py:215
  864.3 92.3 %copy-start.14 = (f32[1536]{0:T(1024)S(1)}, f32[1536]{0:T(1024)}, u32[]{:S(2)}) copy-start(f32[1536]{0:T(1024)} %get-tuple-element.249) | copy-start | bytes 18436
  864.3 161.2 %collective-permute-start.26 = (bf16[20,128,384]{2,1,0:T(8,128)(2,1)}, bf16[20,128,384]{2,1,0:T(8,128)(2,1)}, u32[]{:S(2)}, u32[]{:S(2)}) collective-permute-start(bf16[20,128,384]{2,1,0:T(8,128)(2,1)} %get-tuple-element.299), channel_id=1, source_target_pairs={{0,2},{1,3},{2,0},{3,1},{4,6},{5,7},{6,4},{7,5},{8,10},{9,11},{10,... | collective-permute-start | bytes 5898248 | tf_op jit(solution)/shard_map/ppermute | solution.py:215
  957.9 308.3 %reduce-scatter.11.cloned.1.call-start = ((), (), s32[]{:S(2)}) async-start(), calls=%async_computation.9 | async-start | bytes 7864320 | tf_op jit(solution)/shard_map/reduce_scatter | solution.py:251
  958.0 69.7 %collective-permute-start.19 = (bf16[20,384,128]{2,1,0:T(8,128)(2,1)}, bf16[20,384,128]{2,1,0:T(8,128)(2,1)S(1)}, u32[]{:S(2)}, u32[]{:S(2)}) collective-permute-start(bf16[20,384,128]{2,1,0:T(8,128)(2,1)} %collective-permute-done.18.rest_4_), channel_id=1, source_target_pairs={{0,16},{16,0},{1,17},{17,1},{2,18},{18,2},{3,19},{19,3},{4,20},{20... | collective-permute-start | bytes 5898248 | tf_op jit(solution)/shard_map/ppermute | solution.py:216
  984.1 62.0 %collective-permute-start.23 = (bf16[20,384,128]{2,1,0:T(8,128)(2,1)}, bf16[20,384,128]{2,1,0:T(8,128)(2,1)S(1)}, u32[]{:S(2)}, u32[]{:S(2)}) collective-permute-start(bf16[20,384,128]{2,1,0:T(8,128)(2,1)} %collective-permute-done.22.rest_12_), channel_id=1, source_target_pairs={{0,16},{16,0},{1,17},{17,1},{2,18},{18,2},{3,19},{19,3},{4,20},{20... | collective-permute-start | bytes 5898248 | tf_op jit(solution)/shard_map/ppermute | solution.py:216
  1025.5 61.8 %collective-permute-start.27 = (bf16[20,128,384]{2,1,0:T(8,128)(2,1)}, bf16[20,128,384]{2,1,0:T(8,128)(2,1)S(1)}, u32[]{:S(2)}, u32[]{:S(2)}) collective-permute-start(bf16[20,128,384]{2,1,0:T(8,128)(2,1)} %collective-permute-done.26.rest_20_), channel_id=1, source_target_pairs={{0,16},{16,0},{1,17},{17,1},{2,18},{18,2},{3,19},{19,3},{4,20},{20... | collective-permute-start | bytes 5898248 | tf_op jit(solution)/shard_map/ppermute | solution.py:216
  1027.2 60.1 %collective-permute-start.20 = (bf16[20,384,128]{2,1,0:T(8,128)(2,1)}, bf16[20,384,128]{2,1,0:T(8,128)(2,1)S(1)}, u32[]{:S(2)}, u32[]{:S(2)}) collective-permute-start(bf16[20,384,128]{2,1,0:T(8,128)(2,1)} %collective-permute-done.18.rest_4_), channel_id=1, source_target_pairs={{0,1},{1,0},{2,3},{3,2},{4,5},{5,4},{6,7},{7,6},{8,9},{9,8},{10,11... | collective-permute-start | bytes 5898248 | tf_op jit(solution)/shard_map/ppermute | solution.py:217
  1027.2 60.6 %collective-permute-start.24 = (bf16[20,384,128]{2,1,0:T(8,128)(2,1)}, bf16[20,384,128]{2,1,0:T(8,128)(2,1)S(1)}, u32[]{:S(2)}, u32[]{:S(2)}) collective-permute-start(bf16[20,384,128]{2,1,0:T(8,128)(2,1)} %collective-permute-done.22.rest_12_), channel_id=1, source_target_pairs={{0,1},{1,0},{2,3},{3,2},{4,5},{5,4},{6,7},{7,6},{8,9},{9,8},{10,11... | collective-permute-start | bytes 5898248 | tf_op jit(solution)/shard_map/ppermute | solution.py:217
  1027.7 66.5 %copy-start.28 = (bf16[20,384,128]{2,1,0:T(8,128)(2,1)}, bf16[20,384,128]{2,1,0:T(8,128)(2,1)S(1)}, u32[]{:S(2)}) copy-start(bf16[20,384,128]{2,1,0:T(8,128)(2,1)S(1)} %collective-permute-done.19.rest_5_) | copy-start | bytes 5898244
  1027.7 60.1 %collective-permute-start.28 = (bf16[20,128,384]{2,1,0:T(8,128)(2,1)}, bf16[20,128,384]{2,1,0:T(8,128)(2,1)S(1)}, u32[]{:S(2)}, u32[]{:S(2)}) collective-permute-start(bf16[20,128,384]{2,1,0:T(8,128)(2,1)} %collective-permute-done.26.rest_20_), channel_id=1, source_target_pairs={{0,1},{1,0},{2,3},{3,2},{4,5},{5,4},{6,7},{7,6},{8,9},{9,8},{10,11... | collective-permute-start | bytes 5898248 | tf_op jit(solution)/shard_map/ppermute | solution.py:217
  1046.1 41.7 %collective-permute-start.21 = (bf16[20,384,128]{2,1,0:T(8,128)(2,1)S(1)}, bf16[20,384,128]{2,1,0:T(8,128)(2,1)S(1)}, u32[]{:S(2)}, u32[]{:S(2)}) collective-permute-start(bf16[20,384,128]{2,1,0:T(8,128)(2,1)S(1)} %collective-permute-done.19.rest_5_), channel_id=1, source_target_pairs={{0,1},{1,0},{2,3},{3,2},{4,5},{5,4},{6,7},{7,6},{8,9},{9,8},{10,11... | collective-permute-start | bytes 5898248 | tf_op jit(solution)/shard_map/ppermute | solution.py:218
  1087.3 4.0 collective-permute-start.25
  1087.3 6.9 collective-permute-start.29
  1274.0 74.1 %collective-permute-start.30 = (f32[256,1536]{1,0:T(8,128)S(1)}, f32[256,1536]{1,0:T(8,128)S(1)}, u32[]{:S(2)}, u32[]{:S(2)}) collective-permute-start(f32[256,1536]{1,0:T(8,128)S(1)} %add.154), channel_id=1, source_target_pairs={{0,0},{4,1},{8,2},{12,3},{1,4},{5,5},{9,6},{13,7},{2,8},{6,9},{10,... | collective-permute-start | bytes 4718600 | tf_op jit(solution)/shard_map/ppermute | solution.py:184
  (32 other events, 278.4 us)
Sparse Core Ops, SparseCore 0:
  61.7 62.4 all-gather.17
  135.5 35.7 all-gather.13
  234.9 89.5 reduce-scatter.4
  444.9 67.8 all-gather.19
  571.8 126.0 reduce-scatter.6
  699.3 79.1 all-gather.21
  780.1 25.9 all-gather.15
  862.3 92.5 reduce-scatter.8
  958.1 64.6 all-gather.23
  1153.2 113.0 reduce-scatter.10

commit v2 on v1

--- a/solution.py
+++ b/solution.py
@@ -221,10 +221,12 @@
 
         seg_all = lax.all_gather(seg_ids, ('tok', 'mp'), axis=0)
         pair_info = jnp.concatenate([expert_ids.astype(jnp.float32), expert_gates], axis=1)
-        pair_all = lax.all_gather(pair_info, ('tok', 'mp'), axis=0).reshape(n_tok, n_mp, part_rows, 4)
+        pair_all = lax.all_gather(pair_info, ('tok', 'mp'), axis=0)
+        pair_all = pair_all.reshape(n_tok, n_mp, part_rows, 4)
         seg_full = lax.dynamic_index_in_dim(seg_all.reshape(n_tok, n_mp * part_rows), my_mp, axis=0, keepdims=False)
         pair_mine = lax.dynamic_index_in_dim(pair_all, my_tok, axis=1, keepdims=False).reshape(n_tok * part_rows, 4)
-        route = routing(pair_mine[:, :2].astype(jnp.int32).reshape(-1), pair_mine[:, 2:], num_experts, my_rep, n_tok, part_rows)
+        pair_home = lax.dynamic_index_in_dim(pair_all, my_tok, axis=0, keepdims=False).reshape(n_mp * part_rows, 4)
+        routes = [routing(info[:, :2].astype(jnp.int32).reshape(-1), info[:, 2:], num_experts, my_rep, n_tok, part_rows) for info in (pair_mine, pair_home)]
         seq_len = seg_full.shape[0]
         token_index = jnp.arange(seq_len, dtype=jnp.int32)
         cosines, sines = rope_tables(request_positions(seg_full), head_dim)
@@ -245,11 +247,15 @@
             attn_part = attn_part.reshape(seq_len, hidden_width)
             residual = residual + lax.psum_scatter(attn_part, 'tok', scatter_dimension=0, tiled=True)
             normed = rms_norm(residual, gain_mlp[layer])
+            last = layer == num_layers - 1
+            if last:
+                normed = swap_roles(normed)
+                residual = swap_roles(residual)
             normed = normed.reshape(part_rows, n_tok, slice_width).transpose(1, 0, 2)
             h_all = lax.all_gather(normed, 'mp', axis=0)
-            mix_part = expert_mix(layer, place, route, h_all, layer_sets[layer])
+            mix_part = expert_mix(layer, place, routes[int(last)], h_all, layer_sets[layer])
             mix = lax.psum_scatter(mix_part, 'mp', scatter_dimension=0, tiled=True)
             residual = residual + mix.transpose(1, 0, 2).reshape(part_rows, hidden_width)
-        return swap_roles(residual)
+        return residual
 
     return jax.shard_map(device_step, mesh=mesh, in_specs=in_specs, out_specs=row_spec, check_vma=False)

time: 1360 us -> 1380 us (1.015)
  the two profiles are of different devices: /device:TPU:4 before, /device:TPU:0 now
where the time goes in v2:
time: 1380 us; the launch traced here: 1370 us
  waiting for transfers between devices  810 us (59%)
  blocking collectives  184 us (13%)
  Pallas kernels  119 us (9%)
  matrix products  93.2 us (7%)
  local copies, waits for them, and re-layouts  90 us (7%)
  starting transfers between devices  33.1 us (2%)
  other arithmetic  23.2 us (2%)
  between operations  14.5 us (1%)
    reduce_scatter x2, waiting for transfers between devices, device_step(): mix = lax.psum_scatter(mix_part, 'mp', scatter_dimension=0, tiled=True)  319 us
    ppermute x6, waiting for transfers between devices, device_step(): y_half = lax.ppermute(mine, 'tok', y_perm)  223 us
    all_gather x1, blocking collectives, device_step(): seg_all = lax.all_gather(seg_ids, ('tok', 'mp'), axis=0)  147 us
    pallas_call x2, Pallas kernels, expert_mix(): pl.pallas_call(moe_kernel, grid_spec=pltpu.PrefetchScalarGridSpec(num_sca...  119 us
    reduce_scatter x2, waiting for transfers between devices, device_step(): lax.psum_scatter(attn_part, 'tok', scatter_dimension=0, tiled=True)  90.3 us
    ppermute x6, waiting for transfers between devices, device_step(): x_half = lax.ppermute(y_half, 'rep', x_perm)  79.4 us
    all_gather x2, waiting for transfers between devices, device_step(): pack = lax.all_gather(attn_packs[layer], 'mp', axis=0)  65.3 us
    sub x4, matrix products, one_block(): jax.nn.softmax(jnp.where(allowed, scores, -1e+30), axis=-1)  40.8 us
  transfers between devices with their start and end apart: 42, of which 16 were waited for; matrix products, arithmetic and copies ran while one was open for 6% of the time, Pallas kernels for 0%

profile of v2, /device:TPU:0, one launch (start us, length us, event | category | flops | bytes accessed | tf_op | source)
XLA Modules:
  0.0 1367.1 jit_solution(1796923715822322885)
XLA Ops:
  16.2 147.2 %all-gather.6 = s32[16,1,256]{2,1,0:T(1,128)S(1)} all-gather(s32[1,1,256]{2,1,0:T(1,128)S(1)} %bitcast.279), channel_id=2, replica_groups=mesh['rep'=2,'mp'=4,'tok'=4] {'tok','mp'}, dimensions={0}, use_global_device_ids=true | all-gather | bytes 17408 | tf_op jit(solution)/shard_map/all_gather | solution.py:222
  165.9 4.9 copy.133
  172.5 2.4 copy.134
  174.9 4.7 fusion.82
  186.1 35.7 %while.22 = (s32[]{:T(128)}, bf16[2,512,2,3,64]{1,4,3,2,0:T(8,128)(2,1)}, s32[2,512]{1,0:T(2,128)S(1)}, s32[1024]{0:T(1024)S(1)}, s32[2,512]{1,0:T(2,128)S(1)}, ...) while((s32[]{:T(128)}, ...), condition=%wide.region_6.7_spmd.clone, body=%wide.region_3.6_spmd.clone.sunk | while | flops 825951232 | bytes 27567200 | solution.py:54
  186.7 9.9 fusion.160
  196.5 7.4 fusion.161
  204.5 9.8 fusion.160
  214.4 7.4 fusion.161
  225.8 5.7 fusion.136
  231.5 3.8 dynamic-slice_bitcast_fusion.1
  235.3 5.8 collective-permute-start.8
  241.0 4.5 dynamic-slice_bitcast_fusion
  245.6 4.2 dynamic-slice_bitcast_fusion.2
  251.7 61.5 %collective-permute-done.8.rest_12_ = bf16[20,384,128]{2,1,0:T(8,128)(2,1)S(1)} collective-permute-done((bf16[20,384,128]{2,1,0:T(8,128)(2,1)S(1)}, bf16[20,384,128]{2,1,0:T(8,128)(2,1)S(1)}, u32[]{:S(2)}, u32[]{:S(2)}) %collective-permute-start.8) | collective-permute-done | bytes 1966112 | tf_op jit(solution)/shard_map/ppermute | solution.py:215
  314.5 46.2 %collective-permute-done.13.rest_20_ = bf16[20,128,384]{2,1,0:T(8,128)(2,1)} collective-permute-done((bf16[20,128,384]{2,1,0:T(8,128)(2,1)S(1)}, bf16[20,128,384]{2,1,0:T(8,128)(2,1)}, u32[]{:S(2)}, u32[]{:S(2)}) %collective-permute-start.13) | collective-permute-done | bytes 1966112 | tf_op jit(solution)/shard_map/ppermute | solution.py:215
  362.1 36.9 %collective-permute-done.3.rest_4_ = bf16[20,384,128]{2,1,0:T(8,128)(2,1)S(1)} collective-permute-done((bf16[20,384,128]{2,1,0:T(8,128)(2,1)S(1)}, bf16[20,384,128]{2,1,0:T(8,128)(2,1)S(1)}, u32[]{:S(2)}, u32[]{:S(2)}) %collective-permute-start.3) | collective-permute-done | bytes 1966112 | tf_op jit(solution)/shard_map/ppermute | solution.py:215
  401.6 39.0 %collective-permute-done.4.rest_5_ = bf16[20,384,128]{2,1,0:T(8,128)(2,1)S(1)} collective-permute-done((bf16[20,384,128]{2,1,0:T(8,128)(2,1)S(1)}, bf16[20,384,128]{2,1,0:T(8,128)(2,1)S(1)}, u32[]{:S(2)}, u32[]{:S(2)}) %collective-permute-start.4) | collective-permute-done | bytes 1966112 | tf_op jit(solution)/shard_map/ppermute | solution.py:216
  446.3 3.7 collective-permute-done.5.rest_6_
  450.1 2.7 collective-permute-done.11.rest_15_
  454.3 37.1 %all-gather.2 = f32[4096,4]{0,1:T(4,128)S(1)} all-gather(f32[256,4]{0,1:T(4,128)S(1)} %pad_maximum_fusion.6), channel_id=4, replica_groups=mesh['rep'=2,'mp'=4,'tok'=4] {'tok','mp'}, dimensions={0}, use_global_device_ids=true | all-gather | bytes 69632 | tf_op jit(solution)/shard_map/all_gather | solution.py:224
  500.0 13.8 %all-gather.20.cloned.1.call-done = bf16[16,256,384]{2,1,0:T(8,128)(2,1)} async-done(((bf16[4,256,384]{2,1,0:T(8,128)(2,1)}), bf16[16,256,384]{2,1,0:T(8,128)(2,1)}) %all-gather.20.cloned.1.call-update) | async-done | bytes 3145744 | tf_op jit(solution)/shard_map/all_gather | solution.py:255
  513.8 59.5 %expert_mix.2 = f32[16,256,384]{2,1,0:T(8,128)} custom-call(s32[2]{0:T(128)} %pad_add_fusion.place_ref, s32[40]{0:T(128)} %copy-done.33, s32[40]{0:T(128)} %get-tuple-element.329.count_ref, s32[2048]{0:T(1024)} %copy-done.19, f32[2048]{0:T(1024)} %reshape.326.gate_ref, s32[4,1,256]{2,1,0:T(1,128)} %bitcast.276, s32[4,1,256]{2,1,0:T(1,128)} %bitcast.278, ...), custom_call_target="tpu_custom_call" | custom-call | flops 45097156608 | bytes 60000000 | tf_op jit(solution)/shard_map/expert_mix/pallas_call | solution.py:136
  576.7 130.5 %reduce-scatter.7.cloned.1.call-done = f32[4,256,384]{2,1,0:T(8,128)} async-done(((f32[16,256,384]{2,1,0:T(8,128)}), f32[4,256,384]{2,1,0:T(8,128)}) %reduce-scatter.7.cloned.1.call-update) | async-done | bytes 1572880 | tf_op jit(solution)/shard_map/reduce_scatter | solution.py:257
  714.1 65.3 %all-gather.22.cloned.1.call-done = bf16[1536,1024]{0,1:T(8,128)(2,1)} async-done(((bf16[384,1024]{0,1:T(8,128)(2,1)}), bf16[1536,1024]{0,1:T(8,128)(2,1)}) %all-gather.22.cloned.1.call-update) | async-done | bytes 3145744 | tf_op jit(solution)/shard_map/all_gather | solution.py:234
  779.4 4.7 copy.145
  784.1 3.1 slice.175
  787.3 4.0 copy.146
  795.4 12.7 all-gather.16.cloned.1.call-done
  808.1 4.8 fusion.80
  815.6 2.6 reshape_reshape.14
  820.1 37.3 %while.23 = (s32[]{:T(128)}, bf16[2,512,2,3,64]{1,4,3,2,0:T(8,128)(2,1)}, s32[2,512]{1,0:T(2,128)S(1)}, s32[1024]{0:T(1024)S(1)}, s32[2,512]{1,0:T(2,128)S(1)}, ...) while((s32[]{:T(128)}, ...), condition=%wide.region_17.18_spmd.clone, body=%wide.region_14.17_spmd.clone.sunk | while | flops 825951232 | bytes 28619900 | solution.py:54
  820.8 10.5 fusion.166
  831.3 7.4 fusion.167
  839.3 10.5 fusion.166
  849.9 7.4 fusion.167
  859.5 4.5 fusion.137
  866.5 90.3 %reduce-scatter.9.cloned.1.call-done = f32[256,1536]{1,0:T(8,128)} async-done(((f32[1024,1536]{1,0:T(8,128)}), f32[256,1536]{1,0:T(8,128)}) %reduce-scatter.9.cloned.1.call-update) | async-done | bytes 1572880 | tf_op jit(solution)/shard_map/reduce_scatter | solution.py:248
  962.1 38.7 %collective-permute-done.24.rest_12_ = bf16[20,384,128]{2,1,0:T(8,128)(2,1)} collective-permute-done((bf16[20,384,128]{2,1,0:T(8,128)(2,1)}, bf16[20,384,128]{2,1,0:T(8,128)(2,1)}, u32[]{:S(2)}, u32[]{:S(2)}) %collective-permute-start.24) | collective-permute-done | bytes 1966112 | tf_op jit(solution)/shard_map/ppermute | solution.py:215
  1002.4 39.7 %collective-permute-done.28.rest_20_ = bf16[20,128,384]{2,1,0:T(8,128)(2,1)} collective-permute-done((bf16[20,128,384]{2,1,0:T(8,128)(2,1)}, bf16[20,128,384]{2,1,0:T(8,128)(2,1)}, u32[]{:S(2)}, u32[]{:S(2)}) %collective-permute-start.28) | collective-permute-done | bytes 1966112 | tf_op jit(solution)/shard_map/ppermute | solution.py:215
  1044.3 2.4 collective-permute-done.25.rest_13_
  1046.7 4.1 collective-permute-start.23
  1050.8 38.0 %collective-permute-done.29.rest_21_ = bf16[20,128,384]{2,1,0:T(8,128)(2,1)} collective-permute-done((bf16[20,128,384]{2,1,0:T(8,128)(2,1)}, bf16[20,128,384]{2,1,0:T(8,128)(2,1)}, u32[]{:S(2)}, u32[]{:S(2)}) %collective-permute-start.29) | collective-permute-done | bytes 1966112 | tf_op jit(solution)/shard_map/ppermute | solution.py:216
  1100.1 59.4 %expert_mix.3 = f32[16,256,384]{2,1,0:T(8,128)} custom-call(s32[2]{0:T(128)} %pad_add_fusion.place_ref, s32[40]{0:T(128)} %copy-done.32, s32[40]{0:T(128)} %get-tuple-element.327.count_ref, s32[2048]{0:T(1024)} %copy-done.18, f32[2048]{0:T(1024)} %reshape.333.gate_ref, s32[4,1,256]{2,1,0:T(1,128)} %bitcast.275, s32[4,1,256]{2,1,0:T(1,128)} %bitcast.277, ...), custom_call_target="tpu_custom_call" | custom-call | flops 45097156608 | bytes 60000000 | tf_op jit(solution)/shard_map/expert_mix/pallas_call | solution.py:136
  1162.7 188.1 %reduce-scatter.11.cloned.1.call-done = f32[4,256,384]{2,1,0:T(8,128)} async-done(((f32[16,256,384]{2,1,0:T(8,128)}), f32[4,256,384]{2,1,0:T(8,128)}) %reduce-scatter.11.cloned.1.call-update) | async-done | bytes 1572880 | tf_op jit(solution)/shard_map/reduce_scatter | solution.py:257
  1350.8 3.0 copy.154
  1353.9 3.0 copy.155
  1356.9 3.2 add.198
  (258 shorter events, 96.4 us)
Async XLA Ops:
  6.5 159.3 %all-gather.18.cloned.1.call-start = ((), (), s32[]{:S(2)}) async-start(), calls=%async_computation.10 | async-start | bytes 3932160 | tf_op jit(solution)/shard_map/all_gather | solution.py:234
  11.7 0.7 collective-permute-start.1
  13.3 161.6 %all-gather.14.cloned.1.call-start = ((), (), s32[]{:S(2)}) async-start(), calls=%async_computation.4 | async-start | bytes 3932160 | tf_op jit(solution)/shard_map/all_gather | solution.py:238
  13.4 1.4 collective-permute-start
  16.1 426.4 %reduce-scatter.5.cloned.1.call-start = ((), (), s32[]{:S(2)}) async-start(), calls=%async_computation.5 | async-start | bytes 7864320 | tf_op jit(solution)/shard_map/reduce_scatter | solution.py:248
  231.5 282.3 %all-gather.20.cloned.1.call-start = ((), (), s32[]{:S(2)}) async-start(), calls=%async_computation.11 | async-start | bytes 3932160 | tf_op jit(solution)/shard_map/all_gather | solution.py:255
  235.3 78.0 %collective-permute-start.8 = (bf16[20,384,128]{2,1,0:T(8,128)(2,1)S(1)}, bf16[20,384,128]{2,1,0:T(8,128)(2,1)S(1)}, u32[]{:S(2)}, u32[]{:S(2)}) collective-permute-start(bf16[20,384,128]{2,1,0:T(8,128)(2,1)S(1)} %get-tuple-element.302), channel_id=1, source_target_pairs={{0,2},{1,3},{2,0},{3,1},{4,6},{5,7},{6,4},{7,5},{8,10},{9,11},{10,... | collective-permute-start | bytes 5898248 | tf_op jit(solution)/shard_map/ppermute | solution.py:215
  245.6 196.3 %copy-start.17 = (bf16[2,1536]{1,0:T(2,128)(2,1)S(1)}, bf16[2,1536]{1,0:T(2,128)(2,1)}, u32[]{:S(2)}) copy-start(bf16[2,1536]{1,0:T(2,128)(2,1)} %param.29) | copy-start | bytes 18436
  245.6 115.1 %collective-permute-start.13 = (bf16[20,128,384]{2,1,0:T(8,128)(2,1)S(1)}, bf16[20,128,384]{2,1,0:T(8,128)(2,1)}, u32[]{:S(2)}, u32[]{:S(2)}) collective-permute-start(bf16[20,128,384]{2,1,0:T(8,128)(2,1)S(1)} %get-tuple-element.300), channel_id=1, source_target_pairs={{0,2},{1,3},{2,0},{3,1},{4,6},{5,7},{6,4},{7,5},{8,10},{9,11},{10,... | collective-permute-start | bytes 5898248 | tf_op jit(solution)/shard_map/ppermute | solution.py:215
  249.7 149.3 %collective-permute-start.3 = (bf16[20,384,128]{2,1,0:T(8,128)(2,1)S(1)}, bf16[20,384,128]{2,1,0:T(8,128)(2,1)S(1)}, u32[]{:S(2)}, u32[]{:S(2)}) collective-permute-start(bf16[20,384,128]{2,1,0:T(8,128)(2,1)S(1)} %get-tuple-element.304), channel_id=1, source_target_pairs={{0,2},{1,3},{2,0},{3,1},{4,6},{5,7},{6,4},{7,5},{8,10},{9,11},{10,... | collective-permute-start | bytes 5898248 | tf_op jit(solution)/shard_map/ppermute | solution.py:215
  313.2 131.4 %copy-start.23 = (bf16[20,384,128]{2,1,0:T(8,128)(2,1)}, bf16[20,384,128]{2,1,0:T(8,128)(2,1)S(1)}, u32[]{:S(2)}) copy-start(bf16[20,384,128]{2,1,0:T(8,128)(2,1)S(1)} %collective-permute-done.8.rest_12_) | copy-start | bytes 5898244
  313.2 87.8 %collective-permute-start.9 = (bf16[20,384,128]{2,1,0:T(8,128)(2,1)S(1)}, bf16[20,384,128]{2,1,0:T(8,128)(2,1)S(1)}, u32[]{:S(2)}, u32[]{:S(2)}) collective-permute-start(bf16[20,384,128]{2,1,0:T(8,128)(2,1)S(1)} %collective-permute-done.8.rest_12_), channel_id=1, source_target_pairs={{0,16},{16,0},{1,17},{17,1},{2,18},{18,2},{3,19},{19,3},{4,20},{20... | collective-permute-start | bytes 5898248 | tf_op jit(solution)/shard_map/ppermute | solution.py:216
  360.7 40.5 %collective-permute-start.14 = (bf16[20,128,384]{2,1,0:T(8,128)(2,1)}, bf16[20,128,384]{2,1,0:T(8,128)(2,1)S(1)}, u32[]{:S(2)}, u32[]{:S(2)}) collective-permute-start(bf16[20,128,384]{2,1,0:T(8,128)(2,1)} %collective-permute-done.13.rest_20_), channel_id=1, source_target_pairs={{0,16},{16,0},{1,17},{17,1},{2,18},{18,2},{3,19},{19,3},{4,20},{20... | collective-permute-start | bytes 5898248 | tf_op jit(solution)/shard_map/ppermute | solution.py:216
  399.0 41.5 %copy-start.24 = (bf16[20,384,128]{2,1,0:T(8,128)(2,1)}, bf16[20,384,128]{2,1,0:T(8,128)(2,1)S(1)}, u32[]{:S(2)}) copy-start(bf16[20,384,128]{2,1,0:T(8,128)(2,1)S(1)} %collective-permute-done.3.rest_4_) | copy-start | bytes 5898244
  399.0 41.5 %collective-permute-start.4 = (bf16[20,384,128]{2,1,0:T(8,128)(2,1)S(1)}, bf16[20,384,128]{2,1,0:T(8,128)(2,1)S(1)}, u32[]{:S(2)}, u32[]{:S(2)}) collective-permute-start(bf16[20,384,128]{2,1,0:T(8,128)(2,1)S(1)} %collective-permute-done.3.rest_4_), channel_id=1, source_target_pairs={{0,16},{16,0},{1,17},{17,1},{2,18},{18,2},{3,19},{19,3},{4,20},{20... | collective-permute-start | bytes 5898248 | tf_op jit(solution)/shard_map/ppermute | solution.py:216
  400.5 99.4 %collective-permute-start.12 = (bf16[2,40,128,384]{3,2,1,0:T(8,128)(2,1)}, bf16[2,40,128,384]{3,2,1,0:T(8,128)(2,1)}, u32[]{:S(2)}, u32[]{:S(2)}) collective-permute-start(bf16[2,40,128,384]{3,2,1,0:T(8,128)(2,1)} %rest_17_.3), channel_id=1, source_target_pairs={{0,1},{1,0},{2,3},{3,2},{4,5},{5,4},{6,7},{7,6},{8,9},{9,8},{10,11... | collective-permute-start | bytes 23592968 | tf_op jit(solution)/shard_map/ppermute | solution.py:209
  400.5 99.4 %collective-permute-start.2 = (bf16[2,40,384,128]{3,2,1,0:T(8,128)(2,1)}, bf16[2,40,384,128]{3,2,1,0:T(8,128)(2,1)}, u32[]{:S(2)}, u32[]{:S(2)}) collective-permute-start(bf16[2,40,384,128]{3,2,1,0:T(8,128)(2,1)} %rest_1_.3), channel_id=1, source_target_pairs={{0,1},{1,0},{2,3},{3,2},{4,5},{5,4},{6,7},{7,6},{8,9},{9,8},{10,11... | collective-permute-start | bytes 23592968 | tf_op jit(solution)/shard_map/ppermute | solution.py:209
  401.0 39.5 %copy-start.25 = (bf16[20,384,128]{2,1,0:T(8,128)(2,1)}, bf16[20,384,128]{2,1,0:T(8,128)(2,1)S(1)}, u32[]{:S(2)}) copy-start(bf16[20,384,128]{2,1,0:T(8,128)(2,1)S(1)} %collective-permute-done.9.rest_13_) | copy-start | bytes 5898244
  401.0 98.9 %collective-permute-start.7 = (bf16[2,40,384,128]{3,2,1,0:T(8,128)(2,1)}, bf16[2,40,384,128]{3,2,1,0:T(8,128)(2,1)}, u32[]{:S(2)}, u32[]{:S(2)}) collective-permute-start(bf16[2,40,384,128]{3,2,1,0:T(8,128)(2,1)} %rest_9_.3), channel_id=1, source_target_pairs={{0,1},{1,0},{2,3},{3,2},{4,5},{5,4},{6,7},{7,6},{8,9},{9,8},{10,11... | collective-permute-start | bytes 23592968 | tf_op jit(solution)/shard_map/ppermute | solution.py:209
  401.1 39.4 %copy-start.26 = (bf16[20,128,384]{2,1,0:T(8,128)(2,1)}, bf16[20,128,384]{2,1,0:T(8,128)(2,1)S(1)}, u32[]{:S(2)}) copy-start(bf16[20,128,384]{2,1,0:T(8,128)(2,1)S(1)} %collective-permute-done.14.rest_21_) | copy-start | bytes 5898244
  401.1 44.6 %collective-permute-start.10 = (bf16[20,384,128]{2,1,0:T(8,128)(2,1)S(1)}, bf16[20,384,128]{2,1,0:T(8,128)(2,1)}, u32[]{:S(2)}, u32[]{:S(2)}) collective-permute-start(bf16[20,384,128]{2,1,0:T(8,128)(2,1)S(1)} %collective-permute-done.8.rest_12_), channel_id=1, source_target_pairs={{0,1},{1,0},{2,3},{3,2},{4,5},{5,4},{6,7},{7,6},{8,9},{9,8},{10,11... | collective-permute-start | bytes 5898248 | tf_op jit(solution)/shard_map/ppermute | solution.py:217
  440.5 5.3 collective-permute-start.15
  445.7 261.5 %reduce-scatter.7.cloned.1.call-start = ((), (), s32[]{:S(2)}) async-start(), calls=%async_computation.6 | async-start | bytes 7864320 | tf_op jit(solution)/shard_map/reduce_scatter | solution.py:257
  445.7 4.2 collective-permute-start.5
  445.8 7.0 collective-permute-start.11
  450.0 50.0 %collective-permute-start.16 = (bf16[20,128,384]{2,1,0:T(8,128)(2,1)}, bf16[20,128,384]{2,1,0:T(8,128)(2,1)}, u32[]{:S(2)}, u32[]{:S(2)}) collective-permute-start(bf16[20,128,384]{2,1,0:T(8,128)(2,1)} %copy-done.26), channel_id=1, source_target_pairs={{0,1},{1,0},{2,3},{3,2},{4,5},{5,4},{6,7},{7,6},{8,9},{9,8},{10,11... | collective-permute-start | bytes 5898248 | tf_op jit(solution)/shard_map/ppermute | solution.py:218
  454.1 45.8 %collective-permute-start.6 = (bf16[20,384,128]{2,1,0:T(8,128)(2,1)}, bf16[20,384,128]{2,1,0:T(8,128)(2,1)}, u32[]{:S(2)}, u32[]{:S(2)}) collective-permute-start(bf16[20,384,128]{2,1,0:T(8,128)(2,1)} %copy-done.27), channel_id=1, source_target_pairs={{0,1},{1,0},{2,3},{3,2},{4,5},{5,4},{6,7},{7,6},{8,9},{9,8},{10,11... | collective-permute-start | bytes 5898248 | tf_op jit(solution)/shard_map/ppermute | solution.py:218
  573.3 206.1 %all-gather.22.cloned.1.call-start = ((), (), s32[]{:S(2)}) async-start(), calls=%async_computation.12 | async-start | bytes 3932160 | tf_op jit(solution)/shard_map/all_gather | solution.py:234
  574.6 0.7 collective-permute-start.17
  576.2 231.9 %all-gather.16.cloned.1.call-start = ((), (), s32[]{:S(2)}) async-start(), calls=%async_computation.7 | async-start | bytes 3932160 | tf_op jit(solution)/shard_map/all_gather | solution.py:238
  714.1 242.8 %reduce-scatter.9.cloned.1.call-start = ((), (), s32[]{:S(2)}) async-start(), calls=%async_computation.8 | async-start | bytes 7864320 | tf_op jit(solution)/shard_map/reduce_scatter | solution.py:248
  864.0 236.0 %all-gather.24.cloned.1.call-start = ((), (), s32[]{:S(2)}) async-start(), calls=%async_computation.13 | async-start | bytes 3932160 | tf_op jit(solution)/shard_map/all_gather | solution.py:255
  864.1 96.4 %collective-permute-start.20 = (bf16[20,384,128]{2,1,0:T(8,128)(2,1)}, bf16[20,384,128]{2,1,0:T(8,128)(2,1)}, u32[]{:S(2)}, u32[]{:S(2)}) collective-permute-start(bf16[20,384,128]{2,1,0:T(8,128)(2,1)} %get-tuple-element.303), channel_id=1, source_target_pairs={{0,2},{1,3},{2,0},{3,1},{4,6},{5,7},{6,4},{7,5},{8,10},{9,11},{10,... | collective-permute-start | bytes 5898248 | tf_op jit(solution)/shard_map/ppermute | solution.py:215
  864.5 136.2 %collective-permute-start.24 = (bf16[20,384,128]{2,1,0:T(8,128)(2,1)}, bf16[20,384,128]{2,1,0:T(8,128)(2,1)}, u32[]{:S(2)}, u32[]{:S(2)}) collective-permute-start(bf16[20,384,128]{2,1,0:T(8,128)(2,1)} %get-tuple-element.301), channel_id=1, source_target_pairs={{0,2},{1,3},{2,0},{3,1},{4,6},{5,7},{6,4},{7,5},{8,10},{9,11},{10,... | collective-permute-start | bytes 5898248 | tf_op jit(solution)/shard_map/ppermute | solution.py:215
  866.2 92.3 %copy-start.15 = (f32[1536]{0:T(1024)S(1)}, f32[1536]{0:T(1024)}, u32[]{:S(2)}) copy-start(f32[1536]{0:T(1024)} %get-tuple-element.249) | copy-start | bytes 18436
  866.2 175.9 %collective-permute-start.28 = (bf16[20,128,384]{2,1,0:T(8,128)(2,1)}, bf16[20,128,384]{2,1,0:T(8,128)(2,1)}, u32[]{:S(2)}, u32[]{:S(2)}) collective-permute-start(bf16[20,128,384]{2,1,0:T(8,128)(2,1)} %get-tuple-element.299), channel_id=1, source_target_pairs={{0,2},{1,3},{2,0},{3,1},{4,6},{5,7},{6,4},{7,5},{8,10},{9,11},{10,... | collective-permute-start | bytes 5898248 | tf_op jit(solution)/shard_map/ppermute | solution.py:215
  958.7 0.7 collective-permute-start.19
  960.5 390.4 %reduce-scatter.11.cloned.1.call-start = ((), (), s32[]{:S(2)}) async-start(), calls=%async_computation.9 | async-start | bytes 7864320 | tf_op jit(solution)/shard_map/reduce_scatter | solution.py:257
  960.5 83.8 %collective-permute-start.21 = (bf16[20,384,128]{2,1,0:T(8,128)(2,1)}, bf16[20,384,128]{2,1,0:T(8,128)(2,1)}, u32[]{:S(2)}, u32[]{:S(2)}) collective-permute-start(bf16[20,384,128]{2,1,0:T(8,128)(2,1)} %collective-permute-done.20.rest_4_), channel_id=1, source_target_pairs={{0,16},{16,0},{1,17},{17,1},{2,18},{18,2},{3,19},{19,3},{4,20},{20... | collective-permute-start | bytes 5898248 | tf_op jit(solution)/shard_map/ppermute | solution.py:216
  1000.7 46.0 %collective-permute-start.25 = (bf16[20,384,128]{2,1,0:T(8,128)(2,1)}, bf16[20,384,128]{2,1,0:T(8,128)(2,1)}, u32[]{:S(2)}, u32[]{:S(2)}) collective-permute-start(bf16[20,384,128]{2,1,0:T(8,128)(2,1)} %collective-permute-done.24.rest_12_), channel_id=1, source_target_pairs={{0,16},{16,0},{1,17},{17,1},{2,18},{18,2},{3,19},{19,3},{4,20},{20... | collective-permute-start | bytes 5898248 | tf_op jit(solution)/shard_map/ppermute | solution.py:216
  1042.1 46.7 %collective-permute-start.29 = (bf16[20,128,384]{2,1,0:T(8,128)(2,1)}, bf16[20,128,384]{2,1,0:T(8,128)(2,1)}, u32[]{:S(2)}, u32[]{:S(2)}) collective-permute-start(bf16[20,128,384]{2,1,0:T(8,128)(2,1)} %collective-permute-done.28.rest_20_), channel_id=1, source_target_pairs={{0,16},{16,0},{1,17},{17,1},{2,18},{18,2},{3,19},{19,3},{4,20},{20... | collective-permute-start | bytes 5898248 | tf_op jit(solution)/shard_map/ppermute | solution.py:216
  1043.8 46.9 %collective-permute-start.22 = (bf16[20,384,128]{2,1,0:T(8,128)(2,1)}, bf16[20,384,128]{2,1,0:T(8,128)(2,1)S(1)}, u32[]{:S(2)}, u32[]{:S(2)}) collective-permute-start(bf16[20,384,128]{2,1,0:T(8,128)(2,1)} %collective-permute-done.20.rest_4_), channel_id=1, source_target_pairs={{0,1},{1,0},{2,3},{3,2},{4,5},{5,4},{6,7},{7,6},{8,9},{9,8},{10,11... | collective-permute-start | bytes 5898248 | tf_op jit(solution)/shard_map/ppermute | solution.py:217
  1043.8 56.2 %collective-permute-start.26 = (bf16[20,384,128]{2,1,0:T(8,128)(2,1)}, bf16[20,384,128]{2,1,0:T(8,128)(2,1)}, u32[]{:S(2)}, u32[]{:S(2)}) collective-permute-start(bf16[20,384,128]{2,1,0:T(8,128)(2,1)} %collective-permute-done.24.rest_12_), channel_id=1, source_target_pairs={{0,1},{1,0},{2,3},{3,2},{4,5},{5,4},{6,7},{7,6},{8,9},{9,8},{10,11... | collective-permute-start | bytes 5898248 | tf_op jit(solution)/shard_map/ppermute | solution.py:217
  1044.3 55.7 %collective-permute-start.30 = (bf16[20,128,384]{2,1,0:T(8,128)(2,1)}, bf16[20,128,384]{2,1,0:T(8,128)(2,1)}, u32[]{:S(2)}, u32[]{:S(2)}) collective-permute-start(bf16[20,128,384]{2,1,0:T(8,128)(2,1)} %collective-permute-done.28.rest_20_), channel_id=1, source_target_pairs={{0,1},{1,0},{2,3},{3,2},{4,5},{5,4},{6,7},{7,6},{8,9},{9,8},{10,11... | collective-permute-start | bytes 5898248 | tf_op jit(solution)/shard_map/ppermute | solution.py:217
  1046.7 53.3 %collective-permute-start.23 = (bf16[20,384,128]{2,1,0:T(8,128)(2,1)}, bf16[20,384,128]{2,1,0:T(8,128)(2,1)}, u32[]{:S(2)}, u32[]{:S(2)}) collective-permute-start(bf16[20,384,128]{2,1,0:T(8,128)(2,1)} %collective-permute-done.21.rest_5_), channel_id=1, source_target_pairs={{0,1},{1,0},{2,3},{3,2},{4,5},{5,4},{6,7},{7,6},{8,9},{9,8},{10,11... | collective-permute-start | bytes 5898248 | tf_op jit(solution)/shard_map/ppermute | solution.py:218
  1088.9 11.2 collective-permute-start.27
  1092.0 8.0 collective-permute-start.31
  1160.9 196.0 %collective-permute-start.18 = (f32[256,1536]{1,0:T(8,128)S(1)}, f32[256,1536]{1,0:T(8,128)}, u32[]{:S(2)}, u32[]{:S(2)}) collective-permute-start(f32[256,1536]{1,0:T(8,128)S(1)} %copy-done.2), channel_id=1, source_target_pairs={{0,0},{4,1},{8,2},{12,3},{1,4},{5,5},{9,6},{13,7},{2,8},{6,9},{10,... | collective-permute-start | bytes 4718600 | tf_op jit(solution)/shard_map/ppermute | solution.py:184
  (29 other events, 112.2 us)
Sparse Core Ops, SparseCore 0:
  13.4 130.8 all-gather.17
  145.9 28.0 all-gather.13
  231.6 95.0 reduce-scatter.4
  445.8 67.9 all-gather.19
  573.5 133.6 reduce-scatter.6
  708.6 70.7 all-gather.21
  781.0 27.0 all-gather.15
  864.1 92.6 reduce-scatter.8
  960.6 101.6 all-gather.23
  1159.6 191.1 reduce-scatter.10
